TPU v7x, 32 devices: a whole 2x2x4 slice. The times are simulated.
32 devices in a mesh: dp: 4 (over y, x), ctx: 8 (over z, core).
Axes of the slice: x: 2, y: 2, z: 4, core: 2. Of those that a mesh axis runs over, the one named last changes fastest.
Arguments:
- query: bfloat16 [4, 1024, 4096], P('dp', 'ctx'), may hold values from -6 to 6
- key: bfloat16 [4, 1024, 256], P('dp', 'ctx'), may hold values from -6 to 6
- value: bfloat16 [4, 1024, 256], P('dp', 'ctx'), may hold values from -6 to 6
- span_order: int32 [4, 16], P('dp'), may hold values from 0 to 15, each once within a row
- expert_ids: int32 [4, 1024, 8], P('dp', 'ctx'), may hold values from 0 to 127, as said below
- expert_gates: float32 [4, 1024, 8], P('dp', 'ctx'), may hold values from 0.02 to 0.2
- trainable: int32 [8], replicated, may hold values from 0 to 127, as said below
- norm_gain: float32 [4096], replicated, may hold values from 0.5 to 1.5
- upstream: bfloat16 [4, 1024, 4096], P('dp', 'ctx'), may hold values from -6 to 6
- expert_weights: bfloat16 [8, 768, 3, 4096], P('ctx'), may hold values from -0.09375 to 0.09375
Outputs:
- d_query: bfloat16 [4, 1024, 4096], P('dp', 'ctx')
- key_gradient: bfloat16 [4, 1024, 256], P('dp', 'ctx')
- value_gradient: bfloat16 [4, 1024, 256], P('dp', 'ctx')
- expert_grads: bfloat16 [8, 768, 3, 4096], P('ctx', 'dp')
Inputs may be any that keep to these rules, and one draw needn't show every extreme that they name: `span_order`: each row is a permutation of the 16 span numbers. `expert_ids`: the 8 numbers of a token are distinct; among the 128 rows of one device (aligned blocks of 128 rows of a document) at most 12 name the same expert. `trainable`: distinct expert numbers.
All inputs are finite; a program needn't handle non-finite values.
Results may differ from a plain program's by a relative error of at most 0.02.
Values may be sent and summed in bfloat16 or wider, within the bound.
No kernel may reach another device: no remote copies, remote signals or barrier semaphores. Data moves between devices by JAX's collectives and lax.ppermute only.
A program may use at most 128 MiB of HBM per device.

v0:
```python
import jax
import jax.numpy as jnp
from jax import lax
from jax.experimental import pallas as pl
from jax.experimental.pallas import tpu as pltpu
from jax.sharding import PartitionSpec as P


HEADS_PER_GROUP = 16
HEAD_SIZE = 128
CAP = 12
EPSILON = 1e-06
MASK_FILLER = -1e30
SCALE = HEAD_SIZE ** (-0.5)
LOG2E = 1.4426950408889634
FOLD = 2
PIECE = FOLD * CAP
STEP_HEADS = 4
F32 = jnp.float32
BF16 = jnp.bfloat16


def mm(a, b):
    return lax.dot_general(a, b, (((1,), (0,)), ((), ())), preferred_element_type=F32)


def mm_t(a, b):
    return lax.dot_general(a, b, (((1,), (1,)), ((), ())), preferred_element_type=F32)


def t_mm(a, b):
    return lax.dot_general(a, b, (((0,), (0,)), ((), ())), preferred_element_type=F32)


def iota(shape, dim):
    return lax.broadcasted_iota(jnp.int32, shape, dim)


def params(*semantics):
    if semantics:
        return pltpu.CompilerParams(dimension_semantics=semantics, vmem_limit_bytes=60 << 20)
    return pltpu.CompilerParams(vmem_limit_bytes=60 << 20)


def whole(shape):
    return pl.BlockSpec(shape, lambda *_: (0,) * len(shape))


SMEM_SPEC = pl.BlockSpec(memory_space=pltpu.SMEM)


def route_kernel(n, rows, width, me_ref, train_ref, ids_ref, gates_ref, up_ref, *outs):
    pick_ref, blocks = outs[0], outs[1:]
    ids = ids_ref[...]
    gates = gates_ref[...]
    me = me_ref[0]
    row_n = iota((n, rows), 0)
    hits = jnp.zeros((n, rows), F32)
    level = jnp.zeros((n, rows), F32)
    for k in range(n):
        j = me + k
        j = jnp.where(j >= n, j - n, j)
        same = ids == train_ref[j]
        hit = jnp.sum(same.astype(F32), axis=0, keepdims=True)
        gate = jnp.sum(jnp.where(same, gates, 0.0), axis=0, keepdims=True)
        hits = jnp.where(row_n == k, hit, hits)
        level = jnp.where(row_n == k, gate, level)
    before = (iota((rows, rows), 0) < iota((rows, rows), 1)).astype(BF16)
    rank = mm(hits.astype(BF16), before)
    place = jnp.where(hits > 0.5, rank, 1e4)
    sub = iota((PIECE, rows), 0)
    slot = jnp.where(sub >= CAP, sub - CAP, sub).astype(F32)
    firsts, seconds, scales = [], [], []
    for k in range(n):
        chosen = place[k : k + 1, :] == slot
        firsts.append(jnp.where(chosen & (sub < CAP), 1.0, 0.0))
        seconds.append(jnp.where(chosen & (sub >= CAP), 1.0, 0.0))
        scales.append(jnp.sum(jnp.where(chosen, level[k : k + 1, :], 0.0), axis=1, keepdims=True))
    first = jnp.concatenate(firsts, axis=0).astype(BF16)
    second = jnp.concatenate(seconds, axis=0).astype(BF16)
    scale = jnp.concatenate(scales, axis=0)
    pick_ref[0] = first
    pick_ref[1] = second
    half = width // FOLD
    chunk = min(512, half)
    for c in range(0, half, chunk):
        picked = mm(first, up_ref[:, c : c + chunk]) + mm(second, up_ref[:, half + c : half + c + chunk])
        picked = (picked * scale).astype(BF16)
        for k in range(n):
            blocks[k][:, c : c + chunk] = picked[k * PIECE : (k + 1) * PIECE]


def route(me, trainable, ids, gates, upstream):
    n = trainable.shape[0]
    rows, width = upstream.shape
    half = width // FOLD
    out_shape = [jax.ShapeDtypeStruct((2, n * PIECE, rows), BF16)] + [
        jax.ShapeDtypeStruct((PIECE, half), BF16) for _ in range(n)
    ]
    outs = pl.pallas_call(
        lambda *refs: route_kernel(n, rows, width, *refs),
        out_shape=out_shape,
        in_specs=[SMEM_SPEC, SMEM_SPEC] + [pl.BlockSpec(memory_space=pltpu.VMEM)] * 3,
        compiler_params=params(),
        cost_estimate=pl.CostEstimate(flops=4 * 10**9, bytes_accessed=2 * 10**6, transcendentals=0),
        name="route",
    )(me, trainable, ids, gates, upstream)
    return outs[0], list(outs[1:])


def unfold_kernel(n, slots, half, *refs):
    blocks, out_ref = refs[:n], refs[n]
    r = iota((slots, n * PIECE), 0)
    s = iota((slots, n * PIECE), 1)
    start = r
    for k in range(1, n):
        start = start + jnp.where(r >= k * CAP, PIECE - CAP, 0)
    chunk = min(512, half)
    for f in range(FOLD):
        select = (s == start + f * CAP).astype(BF16)
        for c in range(0, half, chunk):
            stacked = jnp.concatenate([b[:, c : c + chunk] for b in blocks], axis=0)
            at = f * half + c
            out_ref[:, at : at + chunk] = mm(select, stacked).astype(BF16)


def unfold(blocks):
    n = len(blocks)
    half = blocks[0].shape[1]
    slots = n * CAP
    return pl.pallas_call(
        lambda *refs: unfold_kernel(n, slots, half, *refs),
        out_shape=jax.ShapeDtypeStruct((slots, FOLD * half), BF16),
        compiler_params=params(),
        cost_estimate=pl.CostEstimate(flops=2 * 10**9, bytes_accessed=10**6, transcendentals=0),
        name="unfold",
    )(*blocks)


def forward_kernel(n, rows, width, me_ref, span_ref, *refs):
    kv_refs = refs[:n]
    q_ref, pick_ref, gain_ref = refs[n : n + 3]
    ka_ref, va_ref, kt_ref, vt_ref, exp_ref, inv_ref, mixed_ref, factor_ref = refs[n + 3 : n + 11]
    blocks = refs[n + 11 : n + 11 + n]
    b_ref, all_ref = refs[n + 11 + n :]
    step = pl.program_id(0)
    half_rows = rows // 2
    per_step = STEP_HEADS * HEAD_SIZE
    groups = ka_ref.shape[0]

    @pl.when(step == 0)
    def _():
        me = me_ref[0]
        lane = iota((rows, rows), 1)
        sub = iota((rows, rows), 0)
        lane_half = (lane >= half_rows).astype(jnp.int32)
        sub_half = (sub >= half_rows).astype(jnp.int32)
        lane_in = lane - lane_half * half_rows
        sub_in = sub - sub_half * half_rows
        b_ref[...] = jnp.where((lane_half == sub_half) & (lane_in >= sub_in), MASK_FILLER, 0.0).astype(BF16)
        mine0 = span_ref[0, 2 * me]
        mine1 = span_ref[0, 2 * me + 1]
        lane_span = jnp.where(lane_half == 0, mine0, mine1)
        for b in range(n):
            source = source_of(me, b, n)
            sub_span = jnp.where(sub_half == 0, span_ref[0, 2 * source], span_ref[0, 2 * source + 1])
            hot = ((sub_span == lane_span) & (lane_in == sub_in - 1)) | (
                (sub_span > lane_span) & (lane_in == half_rows - 1)
            )
            hot = jnp.where(hot, 1.0, 0.0).astype(BF16)
            kv = kv_refs[b][...]
            at = slice(b * rows, (b + 1) * rows)
            for g in range(groups):
                key = kv[:, g * HEAD_SIZE : (g + 1) * HEAD_SIZE]
                value = kv[:, (groups + g) * HEAD_SIZE : (groups + g + 1) * HEAD_SIZE]
                ka_ref[g, at, :HEAD_SIZE] = key
                ka_ref[g, at, HEAD_SIZE:] = hot
                va_ref[g, at, :HEAD_SIZE] = value
                va_ref[g, at, HEAD_SIZE:] = jnp.full((rows, HEAD_SIZE), -1.0, BF16)
                kt_ref[g, :, at] = key.T
                vt_ref[g, :HEAD_SIZE, at] = value.T
                vt_ref[g, HEAD_SIZE:, at] = jnp.ones((16, rows), BF16)

    g = step // (HEADS_PER_GROUP // STEP_HEADS)
    b = b_ref[...]
    for p in range(STEP_HEADS // 2):
        at = p * 2 * HEAD_SIZE
        q0 = q_ref[:, at : at + HEAD_SIZE]
        q1 = q_ref[:, at + HEAD_SIZE : at + 2 * HEAD_SIZE]
        qb = jnp.concatenate(
            [jnp.concatenate([q0, b], axis=1), jnp.concatenate([q1, b], axis=1)], axis=0
        )
        scores = mm_t(ka_ref[g], qb)
        peak = jnp.max(scores, axis=0, keepdims=True)
        exps = jnp.exp2((scores - peak) * (SCALE * LOG2E)).astype(BF16)
        exp_ref[p] = exps
        out = mm(vt_ref[g], exps)
        inv = 1.0 / out[HEAD_SIZE : HEAD_SIZE + 1, :]
        normal = out[:HEAD_SIZE, :] * inv
        inv_full = jnp.broadcast_to(inv, (rows, 2 * rows))
        for i in range(2):
            cols = slice(at + i * HEAD_SIZE, at + (i + 1) * HEAD_SIZE)
            head = normal[:, i * rows : (i + 1) * rows].T.astype(BF16)
            mixed_ref[:, cols] = head
            all_ref[step, :, cols] = head
            inv_ref[:, cols] = inv_full[:, i * rows : (i + 1) * rows].T

    @pl.when(step == pl.num_programs(0) - 1)
    def _():
        steps = width // per_step
        square = jnp.zeros((rows, 1), F32)
        for i in range(steps):
            part = all_ref[i].astype(F32)
            square = square + jnp.sum(part * part, axis=1, keepdims=True)
        factor = lax.rsqrt(square / width + EPSILON)
        factor_ref[...] = jnp.broadcast_to(factor, (rows, 128))

        def normed(i):
            gain = gain_ref[:, i * per_step : (i + 1) * per_step]
            return (all_ref[i].astype(F32) * factor * gain).astype(BF16)

        for i in range(steps // FOLD):
            picked = mm(pick_ref[0], normed(i)) + mm(pick_ref[1], normed(steps // FOLD + i))
            picked = picked.astype(BF16)
            for k in range(n):
                blocks[k][:, i * per_step : (i + 1) * per_step] = picked[k * PIECE : (k + 1) * PIECE]


def source_of(me, b, n):
    core = me % 2
    chip = me // 2 - b // 2
    chip = jnp.where(chip < 0, chip + n // 2, chip)
    return 2 * chip + (core if b % 2 == 0 else 1 - core)


def forward(me, span, kv_blocks, query, pick, gain):
    n = len(kv_blocks)
    rows, width = query.shape
    groups = kv_blocks[0].shape[1] // (2 * HEAD_SIZE)
    total = n * rows
    per_step = STEP_HEADS * HEAD_SIZE
    steps = width // per_step
    half = width // FOLD
    pairs = width // (2 * HEAD_SIZE)
    out_shape = [
        jax.ShapeDtypeStruct((groups, total, 2 * HEAD_SIZE), BF16),
        jax.ShapeDtypeStruct((groups, total, 2 * HEAD_SIZE), BF16),
        jax.ShapeDtypeStruct((groups, HEAD_SIZE, total), BF16),
        jax.ShapeDtypeStruct((groups, HEAD_SIZE + 16, total), BF16),
        jax.ShapeDtypeStruct((pairs, total, 2 * rows), BF16),
        jax.ShapeDtypeStruct((rows, width), F32),
        jax.ShapeDtypeStruct((rows, width), BF16),
        jax.ShapeDtypeStruct((rows, 128), F32),
    ] + [jax.ShapeDtypeStruct((PIECE, half), BF16) for _ in range(n)]
    column = pl.BlockSpec((rows, per_step), lambda i: (0, i))
    out_specs = [whole(s.shape) for s in out_shape]
    out_specs[4] = pl.BlockSpec((STEP_HEADS // 2, total, 2 * rows), lambda i: (i, 0, 0))
    out_specs[5] = column
    out_specs[6] = column
    outs = pl.pallas_call(
        lambda *refs: forward_kernel(n, rows, width, *refs),
        out_shape=out_shape,
        grid=(steps,),
        in_specs=[SMEM_SPEC, SMEM_SPEC]
        + [whole(kv_blocks[0].shape)] * n
        + [column, whole(pick.shape), whole(gain.shape)],
        out_specs=out_specs,
        scratch_shapes=[pltpu.VMEM((rows, rows), BF16), pltpu.VMEM((steps, rows, per_step), BF16)],
        compiler_params=params("arbitrary"),
        cost_estimate=pl.CostEstimate(flops=10**10, bytes_accessed=2 * 10**7, transcendentals=4 * 10**6),
        name="forward",
    )(me, span, *kv_blocks, query, pick, gain)
    return outs[:8], list(outs[8:])


def gated(gate_in, up_in, back):
    sigma = 1.0 / (1.0 + jnp.exp(-gate_in))
    act = gate_in * sigma
    grad_gate = (back * up_in * sigma * (1.0 + gate_in * (1.0 - sigma))).astype(BF16)
    grad_up = (back * act).astype(BF16)
    product = (act * up_in).astype(BF16)
    return grad_gate, grad_up, product


def early_kernel(grads_ref, weights, back_ref):
    back_ref[...] = mm_t(grads_ref[...], weights[0])


def early(weighted, weights):
    hidden, width = weights.shape[1:]
    slots = weighted.shape[0]
    tile = 256
    return pl.pallas_call(
        early_kernel,
        out_shape=jax.ShapeDtypeStruct((slots, hidden), F32),
        grid=(hidden // tile,),
        in_specs=[whole(weighted.shape), pl.BlockSpec((1, tile, width), lambda i: (2, i, 0))],
        out_specs=pl.BlockSpec((slots, tile), lambda i: (0, i)),
        compiler_params=params("arbitrary"),
        cost_estimate=pl.CostEstimate(flops=2 * 10**9, bytes_accessed=7 * 10**6, transcendentals=0),
        name="early",
    )(weighted, weights)


def expert_kernel(n, slots, routed_ref, back_ref, weights, *refs):
    blocks, acc_ref = refs[:n], refs[n]
    step = pl.program_id(0)
    width = acc_ref.shape[1]
    routed = routed_ref[...]
    gate_in = mm_t(routed, weights[0])
    up_in = mm_t(routed, weights[1])
    grad_gate, grad_up, _ = gated(gate_in, up_in, back_ref[...])
    got = mm(grad_gate, weights[0]) + mm(grad_up, weights[1])

    @pl.when(step == 0)
    def _():
        acc_ref[...] = got

    @pl.when(step > 0)
    def _():
        acc_ref[...] += got

    @pl.when(step == pl.num_programs(0) - 1)
    def _():
        half = width // FOLD
        r = iota((n * PIECE, slots), 1)
        s = iota((n * PIECE, slots), 0)
        start = r
        for k in range(1, n):
            start = start + jnp.where(r >= k * CAP, PIECE - CAP, 0)
        first = (s == start).astype(BF16)
        second = (s == start + CAP).astype(BF16)
        chunk = min(512, half)
        for c in range(0, half, chunk):
            spread = mm(first, acc_ref[:, c : c + chunk].astype(BF16)) + mm(
                second, acc_ref[:, half + c : half + c + chunk].astype(BF16)
            )
            spread = spread.astype(BF16)
            for k in range(n):
                blocks[k][:, c : c + chunk] = spread[k * PIECE : (k + 1) * PIECE]


def expert(routed, back, weights, n):
    slots = n * CAP
    hidden, width = weights.shape[1:]
    tile = 256
    half = width // FOLD
    return list(
        pl.pallas_call(
            lambda *refs: expert_kernel(n, slots, *refs),
            out_shape=[jax.ShapeDtypeStruct((PIECE, half), BF16)] * n,
            grid=(hidden // tile,),
            in_specs=[
                whole(routed.shape),
                pl.BlockSpec((slots, tile), lambda i: (0, i)),
                pl.BlockSpec((2, tile, width), lambda i: (0, i, 0)),
            ],
            out_specs=[whole((PIECE, half))] * n,
            scratch_shapes=[pltpu.VMEM((slots, width), F32)],
            compiler_params=params("arbitrary"),
            cost_estimate=pl.CostEstimate(flops=8 * 10**9, bytes_accessed=2 * 10**7, transcendentals=0),
            name="expert",
        )(routed, back, weights)
    )


def grads_kernel(count, dp_ref, *refs):
    row_parts, grad_parts = refs[:count], refs[count : 2 * count]
    weights, out_ref, rows_ref, grads_ref, sems = refs[2 * count :]
    part = row_parts[0].shape[0]

    @pl.when(pl.program_id(0) == 0)
    def _():
        copies = []
        for i in range(count):
            at = pl.ds(i * part, part)
            copies.append(pltpu.make_async_copy(row_parts[i], rows_ref.at[at], sems.at[i]))
            copies.append(pltpu.make_async_copy(grad_parts[i], grads_ref.at[at], sems.at[count + i]))
        for copy in copies:
            copy.start()
        for copy in copies:
            copy.wait()

    rows = rows_ref[...]
    grads = grads_ref[...]
    gate_in = mm_t(rows, weights[0])
    up_in = mm_t(rows, weights[1])
    back = mm_t(grads, weights[2])
    grad_gate, grad_up, product = gated(gate_in, up_in, back)
    out_ref[0] = t_mm(grad_gate, rows).astype(BF16)
    out_ref[1] = t_mm(grad_up, rows).astype(BF16)
    out_ref[2] = t_mm(product, grads).astype(BF16)


def expert_gradients(dp_index, row_parts, grad_parts, weights, share):
    count = len(row_parts)
    width = weights.shape[2]
    tile = share
    steps = share // tile
    part = row_parts[0].shape
    return pl.pallas_call(
        lambda *refs: grads_kernel(count, *refs),
        out_shape=jax.ShapeDtypeStruct((3, share, width), BF16),
        grid_spec=pltpu.PrefetchScalarGridSpec(
            num_scalar_prefetch=1,
            grid=(steps,),
            in_specs=[pl.BlockSpec(memory_space=pl.ANY)] * (2 * count)
            + [pl.BlockSpec((3, tile, width), lambda i, d: (0, d[0] * steps + i, 0))],
            out_specs=pl.BlockSpec((3, tile, width), lambda i, d: (0, i, 0)),
            scratch_shapes=[pltpu.VMEM((count * part[0], width), BF16)] * 2
            + [pltpu.SemaphoreType.DMA((2 * count,))],
        ),
        compiler_params=params("arbitrary"),
        cost_estimate=pl.CostEstimate(flops=10**10, bytes_accessed=15 * 10**6, transcendentals=0),
        name="grads",
    )(dp_index, *row_parts, *grad_parts, weights)


def backward_kernel(n, rows, width, *refs):
    back_refs = refs[:n]
    pick_ref, up_ref, mixed_ref, gain_ref, factor_ref, q_ref, inv_ref, exp_ref, va_ref, kt_ref = refs[n : n + 10]
    dq_ref, near_ref, far_ref = refs[n + 10 : n + 13]
    gm_ref, ig_ref, dk_ref, dv_ref = refs[n + 13 :]
    step = pl.program_id(0)
    per_step = STEP_HEADS * HEAD_SIZE
    per_group = HEADS_PER_GROUP // STEP_HEADS
    chunks = width // per_step
    g = step // per_group

    @pl.when(step == 0)
    def _():
        half_chunks = chunks // FOLD
        total = jnp.zeros((rows, 1), F32)
        for i in range(chunks):
            f, c = i // half_chunks, (i % half_chunks) * per_step
            stacked = jnp.concatenate([b[:, c : c + per_step] for b in back_refs], axis=0)
            grad = t_mm(pick_ref[f], stacked) * gain_ref[:, i * per_step : (i + 1) * per_step]
            ig_ref[i] = grad
            mixed = mixed_ref[:, i * per_step : (i + 1) * per_step].astype(F32)
            total = total + jnp.sum(grad * mixed, axis=1, keepdims=True)
        factor = factor_ref[:, :1]
        pull = factor * factor * factor * (total / width)
        for i in range(chunks):
            mixed = mixed_ref[:, i * per_step : (i + 1) * per_step].astype(F32)
            up = up_ref[:, i * per_step : (i + 1) * per_step].astype(F32)
            gm_ref[i] = (up + (factor * ig_ref[i] - mixed * pull)).astype(BF16)

    @pl.when(step % per_group == 0)
    def _():
        dk_ref[...] = jnp.zeros_like(dk_ref)
        dv_ref[...] = jnp.zeros_like(dv_ref)

    col = pl.multiple_of(step * per_step, per_step)
    grad_all = gm_ref[step].astype(F32) * inv_ref[...]
    grad_b = grad_all.astype(BF16)
    prod = (grad_b.astype(F32) * mixed_ref[:, pl.ds(col, per_step)].astype(F32)).astype(BF16)
    for p in range(STEP_HEADS // 2):
        at = p * 2 * HEAD_SIZE

        def stack(x):
            return jnp.concatenate([x[:, at : at + HEAD_SIZE], x[:, at + HEAD_SIZE : at + 2 * HEAD_SIZE]], axis=0)

        gs = stack(grad_b)
        gb = jnp.concatenate([gs, stack(prod)], axis=1)
        pushed = mm_t(va_ref[g], gb)
        exps = exp_ref[p]
        slopes = (exps.astype(F32) * pushed).astype(BF16)
        qs = jnp.concatenate([q_ref[:, at : at + HEAD_SIZE], q_ref[:, at + HEAD_SIZE : at + 2 * HEAD_SIZE]], axis=0)
        dk_ref[...] += mm(slopes, qs)
        dv_ref[...] += mm(exps, gs)
        dq = mm(kt_ref[g], slopes) * SCALE
        for i in range(2):
            cols = slice(at + i * HEAD_SIZE, at + (i + 1) * HEAD_SIZE)
            dq_ref[:, cols] = dq[:, i * rows : (i + 1) * rows].T.astype(BF16)

    groups = va_ref.shape[0]
    for gg in range(groups):

        @pl.when(step == (gg + 1) * per_group - 1)
        def _():
            for b in range(n):
                at = slice(b * rows, (b + 1) * rows)
                kcol = slice(gg * HEAD_SIZE, (gg + 1) * HEAD_SIZE)
                vcol = slice((groups + gg) * HEAD_SIZE, (groups + gg + 1) * HEAD_SIZE)
                if b % 2 == 0:
                    near_ref[b // 2, :, kcol] = dk_ref[at] * SCALE
                    near_ref[b // 2, :, vcol] = dv_ref[at]
                else:
                    far_ref[b // 2, :, kcol] = (dk_ref[at] * SCALE).astype(BF16)
                    far_ref[b // 2, :, vcol] = dv_ref[at].astype(BF16)


def backward(back, pick, upstream, gain, query, fwd):
    _, va, kt, _, exps, inv, mixed, factor = fwd
    n = len(back)
    rows, width = query.shape
    groups, total = va.shape[:2]
    per_step = STEP_HEADS * HEAD_SIZE
    steps = width // per_step
    column = pl.BlockSpec((rows, per_step), lambda i: (0, i))
    kv_width = 2 * groups * HEAD_SIZE
    return pl.pallas_call(
        lambda *refs: backward_kernel(n, rows, width, *refs),
        out_shape=[
            jax.ShapeDtypeStruct((rows, width), BF16),
            jax.ShapeDtypeStruct((n // 2, rows, kv_width), F32),
            jax.ShapeDtypeStruct((n // 2, rows, kv_width), BF16),
        ],
        grid=(steps,),
        in_specs=[whole(back[0].shape)] * n
        + [whole(pick.shape), whole(upstream.shape), whole(mixed.shape), whole(gain.shape), whole(factor.shape)]
        + [
            column,
            column,
            pl.BlockSpec((STEP_HEADS // 2, total, 2 * rows), lambda i: (i, 0, 0)),
            whole(va.shape),
            whole(kt.shape),
        ],
        out_specs=[column, whole((n // 2, rows, kv_width)), whole((n // 2, rows, kv_width))],
        scratch_shapes=[
            pltpu.VMEM((steps, rows, per_step), BF16),
            pltpu.VMEM((steps, rows, per_step), F32),
            pltpu.VMEM((total, HEAD_SIZE), F32),
            pltpu.VMEM((total, HEAD_SIZE), F32),
        ],
        compiler_params=params("arbitrary"),
        cost_estimate=pl.CostEstimate(flops=2 * 10**10, bytes_accessed=2 * 10**7, transcendentals=0),
        name="backward",
    )(*back, pick, upstream, mixed, gain, factor, query, inv, exps, va, kt)


def shift(x, axis, k):
    n = lax.axis_size(axis)
    return lax.ppermute(x, axis, [(i, (i + k) % n) for i in range(n)])


def flip(x, axis, bit):
    n = lax.axis_size(axis)
    return lax.ppermute(x, axis, [(i, i ^ bit) for i in range(n)])


def far_first(n):
    return sorted(range(1, n), key=lambda k: -min(k, n - k))


def exchange(blocks, sign):
    n = len(blocks)
    got = [blocks[0]] + [None] * (n - 1)
    for k in far_first(n):
        got[k] = shift(blocks[k], "ctx", sign * k)
    return got


def gather_docs(rows):
    n = lax.axis_size("dp")
    return [rows] + [flip(rows, "dp", k) for k in range(n - 1, 0, -1)]


def per_device(
    query,
    key,
    value,
    span_order,
    expert_ids,
    expert_gates,
    trainable,
    norm_gain,
    upstream,
    expert_weights,
):
    n = lax.axis_size("ctx")
    chips = n // 2
    me = lax.axis_index("ctx").astype(jnp.int32).reshape(1)
    dp_index = lax.axis_index("dp").astype(jnp.int32).reshape(1)
    weights = expert_weights[0].transpose(1, 0, 2)
    gain = norm_gain[None, :]
    grad_out = upstream[0]

    kv = jnp.concatenate([key[0], value[0]], axis=1)
    arrived = [kv] + [shift(kv, "ctx", 2 * m) for m in range(1, chips)]
    kv_blocks = []
    for block in arrived:
        kv_blocks += [block, flip(block, "ctx", 1)]

    pick, grad_blocks = route(me, trainable, expert_ids[0].T, expert_gates[0].T, grad_out)
    grad_blocks = exchange(grad_blocks, 1)
    weighted = unfold(grad_blocks)
    all_weighted = gather_docs(weighted)
    back_rows = early(weighted, weights)

    fwd, row_blocks = forward(me, span_order, kv_blocks, query[0], pick, gain)
    row_blocks = exchange(row_blocks, 1)
    routed = unfold(row_blocks)
    all_routed = gather_docs(routed)
    returned = expert(routed, back_rows, weights, n)
    back = exchange(returned, -1)
    share = weights.shape[1] // lax.axis_size("dp")
    expert_grads = expert_gradients(dp_index, all_routed, all_weighted, weights, share)
    d_query, near, far = backward(back, pick, grad_out, gain, query[0], fwd)

    far = flip(far, "ctx", 1)
    met = near + far.astype(F32)
    total = met[0]
    sent = met.astype(BF16)
    landed = [shift(sent[m], "ctx", -2 * m) for m in range(1, chips)]
    for block in landed:
        total = total + block.astype(F32)
    split = key.shape[2]
    return (
        d_query[None],
        total[:, :split].astype(BF16)[None],
        total[:, split:].astype(BF16)[None],
        expert_grads.transpose(1, 0, 2)[None],
    )


def solution(mesh):
    in_specs = (
        P("dp", "ctx", None),
        P("dp", "ctx", None),
        P("dp", "ctx", None),
        P("dp", None),
        P("dp", "ctx", None),
        P("dp", "ctx", None),
        P(),
        P(),
        P("dp", "ctx", None),
        P("ctx", None, None, None),
    )
    out_specs = (
        P("dp", "ctx", None),
        P("dp", "ctx", None),
        P("dp", "ctx", None),
        P("ctx", "dp", None, None),
    )

    return jax.shard_map(per_device, mesh=mesh, in_specs=in_specs, out_specs=out_specs, check_vma=False)
```

profile of v0, /device:TPU:0, one launch (start us, length us, event | category | flops | bytes accessed | tf_op | source)
XLA Modules:
  0.0 213.8 jit_solution(15545927251437235341)
XLA Ops:
  1.5 3.1 %collective-permute-start.1 = (bf16[128,512]{1,0:T(8,128)(2,1)S(1)}, bf16[128,512]{1,0:T(8,128)(2,1)S(1)}, u32[]{:S(2)}, u32[]{:S(2)}) collective-permute-start(bf16[128,512]{1,0:T(8,128)(2,1)S(1)} %pad_maximum_fusion.refs_2_), channel_id=1, source_target_pairs={{0,2},{1,3},{2,4},{3,5},{4,6},{5,7},{6,0},{7,1},{8,10},{9,11},{10,... | collective-permute-start | bytes 393224 | tf_op jit(solution)/shard_map/ppermute | solution.py:534
  4.6 2.6 %collective-permute-start.3 = (bf16[128,512]{1,0:T(8,128)(2,1)S(1)}, bf16[128,512]{1,0:T(8,128)(2,1)S(1)}, u32[]{:S(2)}, u32[]{:S(2)}) collective-permute-start(bf16[128,512]{1,0:T(8,128)(2,1)S(1)} %pad_maximum_fusion.refs_2_), channel_id=1, source_target_pairs={{0,4},{1,5},{2,6},{3,7},{4,0},{5,1},{6,2},{7,3},{8,12},{9,13},{10,... | collective-permute-start | bytes 393224 | tf_op jit(solution)/shard_map/ppermute | solution.py:534
  8.6 2.8 %route.1 = (bf16[2,192,128]{2,1,0:T(8,128)(2,1)}, bf16[24,2048]{1,0:T(8,128)(2,1)}, bf16[24,2048]{1,0:T(8,128)(2,1)}, bf16[24,2048]{1,0:T(8,128)(2,1)}, bf16[24,...) custom-call(s32[1]{0:T(128)} %bitcast.refs_0_, ...), custom_call_target="tpu_custom_call" | custom-call | flops 4000000000 | bytes 2000000 | tf_op jit(solution)/shard_map/route/pallas_call | solution.py:100
  12.2 3.6 %collective-permute-done.3.refs_6_ = bf16[128,512]{1,0:T(8,128)(2,1)S(1)} collective-permute-done((bf16[128,512]{1,0:T(8,128)(2,1)S(1)}, bf16[128,512]{1,0:T(8,128)(2,1)S(1)}, u32[]{:S(2)}, u32[]{:S(2)}) %collective-permute-start.3) | collective-permute-done | bytes 131104 | tf_op jit(solution)/shard_map/ppermute | solution.py:534
  17.5 2.7 %collective-permute-start.15 = (bf16[24,2048]{1,0:T(8,128)(2,1)}, bf16[24,2048]{1,0:T(8,128)(2,1)S(1)}, u32[]{:S(2)}, u32[]{:S(2)}) collective-permute-start(bf16[24,2048]{1,0:T(8,128)(2,1)} %get-tuple-element.49), channel_id=1, source_target_pairs={{0,2},{1,3},{2,4},{3,5},{4,6},{5,7},{6,0},{7,1},{8,10},{9,11},{10,... | collective-permute-start | bytes 294920 | tf_op jit(solution)/shard_map/ppermute | solution.py:534
  20.3 4.8 %collective-permute-done.15.refs_2_ = bf16[24,2048]{1,0:T(8,128)(2,1)S(1)} collective-permute-done((bf16[24,2048]{1,0:T(8,128)(2,1)}, bf16[24,2048]{1,0:T(8,128)(2,1)S(1)}, u32[]{:S(2)}, u32[]{:S(2)}) %collective-permute-start.15) | collective-permute-done | bytes 98336 | tf_op jit(solution)/shard_map/ppermute | solution.py:534
  27.8 2.6 %collective-permute-start.19 = (bf16[24,2048]{1,0:T(8,128)(2,1)}, bf16[24,2048]{1,0:T(8,128)(2,1)S(1)}, u32[]{:S(2)}, u32[]{:S(2)}) collective-permute-start(bf16[24,2048]{1,0:T(8,128)(2,1)} %get-tuple-element.53), channel_id=1, source_target_pairs={{0,6},{1,7},{2,0},{3,1},{4,2},{5,3},{6,4},{7,5},{8,14},{9,15},{10,... | collective-permute-start | bytes 294920 | tf_op jit(solution)/shard_map/ppermute | solution.py:534
  31.0 20.3 %forward.1 = (bf16[2,1024,256]{2,1,0:T(8,128)(2,1)}, bf16[2,1024,256]{2,1,0:T(8,128)(2,1)}, bf16[2,128,1024]{2,1,0:T(8,128)(2,1)}, bf16[2,144,1024]{2,1,0:T(8,12...) custom-call(s32[1]{0:T(128)} %bitcast.refs_0_, ...), custom_call_target="tpu_custom_call" | custom-call | flops 10000000000 | bytes 20000000 | tf_op jit(solution)/shard_map/forward/pallas_call | solution.py:260
  52.3 2.5 %unfold.3.grads_ref.refs_5_ = bf16[96,4096]{1,0:T(8,128)(2,1)} custom-call(bf16[24,2048]{1,0:T(8,128)(2,1)} %get-tuple-element.47.refs_0_, bf16[24,2048]{1,0:T(8,128)(2,1)} %copy-done.11, bf16[24,2048]{1,0:T(8,128)(2,1)} %copy-done.12, bf16[24,2048]{1,0:T(8,128)(2,1)} %copy-done.13, bf16[24,2048]{1,0:T(8,128)(2,1)} %copy-done.14, ...), custom_call_target="tpu_custom_call" | custom-call | flops 2000000000 | bytes 1000000 | tf_op jit(solution)/shard_map/unfold/pallas_call | solution.py:131
  62.3 5.6 %early.1.refs_1_ = f32[96,768]{1,0:T(8,128)} custom-call(bf16[96,4096]{1,0:T(8,128)(2,1)} %unfold.3.grads_ref.refs_5_, bf16[3,768,4096]{2,1,0:T(8,128)(2,1)} %bitcast.40), custom_call_target="tpu_custom_call" | custom-call | flops 2000000000 | bytes 7000000 | tf_op jit(solution)/shard_map/early/pallas_call | solution.py:293
  68.8 2.5 %unfold.2.refs_0_.refs_1_ = bf16[96,4096]{1,0:T(8,128)(2,1)} custom-call(bf16[24,2048]{1,0:T(8,128)(2,1)} %get-tuple-element.39.refs_0_, bf16[24,2048]{1,0:T(8,128)(2,1)} %copy-done.15, bf16[24,2048]{1,0:T(8,128)(2,1)} %copy-done.17, bf16[24,2048]{1,0:T(8,128)(2,1)} %copy-done.25, bf16[24,2048]{1,0:T(8,128)(2,1)} %copy-done.27, bf16[24,2048]{1,0:T(8,128)(2,1)} %copy-done.28, ...), custom_call_target="tpu_custom_call" | custom-call | flops 2000000000 | bytes 1000000 | tf_op jit(solution)/shard_map/unfold/pallas_call | solution.py:131
  71.2 11.0 %expert.1 = (bf16[24,2048]{1,0:T(8,128)(2,1)}, bf16[24,2048]{1,0:T(8,128)(2,1)}, bf16[24,2048]{1,0:T(8,128)(2,1)}, bf16[24,2048]{1,0:T(8,128)(2,1)}, bf16[24,204...) custom-call(bf16[96,4096]{1,0:T(8,128)(2,1)} %unfold.2.refs_0_.refs_1_, ...), custom_call_target="tpu_custom_call" | custom-call | flops 8000000000 | bytes 20000000 | tf_op jit(solution)/shard_map/expert/pallas_call | solution.py:349
  82.2 7.1 %collective-permute-start.21 = (bf16[24,2048]{1,0:T(8,128)(2,1)}, bf16[24,2048]{1,0:T(8,128)(2,1)S(1)}, u32[]{:S(2)}, u32[]{:S(2)}) collective-permute-start(bf16[24,2048]{1,0:T(8,128)(2,1)} %get-tuple-element.56), channel_id=1, source_target_pairs={{0,7},{1,0},{2,1},{3,2},{4,3},{5,4},{6,5},{7,6},{8,15},{9,8},{10,9... | collective-permute-start | bytes 294920 | tf_op jit(solution)/shard_map/ppermute | solution.py:534
  89.3 2.7 %collective-permute-start.24 = (bf16[24,2048]{1,0:T(8,128)(2,1)}, bf16[24,2048]{1,0:T(8,128)(2,1)S(1)}, u32[]{:S(2)}, u32[]{:S(2)}) collective-permute-start(bf16[24,2048]{1,0:T(8,128)(2,1)} %get-tuple-element.59), channel_id=1, source_target_pairs={{0,4},{1,5},{2,6},{3,7},{4,0},{5,1},{6,2},{7,3},{8,12},{9,13},{10,... | collective-permute-start | bytes 294920 | tf_op jit(solution)/shard_map/ppermute | solution.py:534
  97.1 9.1 %collective-permute-done.24.refs_4_ = bf16[24,2048]{1,0:T(8,128)(2,1)S(1)} collective-permute-done((bf16[24,2048]{1,0:T(8,128)(2,1)}, bf16[24,2048]{1,0:T(8,128)(2,1)S(1)}, u32[]{:S(2)}, u32[]{:S(2)}) %collective-permute-start.24) | collective-permute-done | bytes 98336 | tf_op jit(solution)/shard_map/ppermute | solution.py:534
  108.1 17.5 %backward.1 = (bf16[128,4096]{1,0:T(8,128)(2,1)}, f32[4,128,512]{2,1,0:T(8,128)}, bf16[4,128,512]{2,1,0:T(8,128)(2,1)}) custom-call(bf16[24,2048]{1,0:T(8,128)(2,1)} %get-tuple-element.55.refs_0_, bf16[24,2048]{1,0:T(8,128)(2,1)} %copy-done.19, bf16[24,2048]{1,0:T(8,128)(2,1)} %copy-done.21, bf16[24,2048]{1,0:T(8,128)(2,1)} %copy-done.22, ...), custom_call_target="tpu_custom_call" | custom-call | flops 20000000000 | bytes 20000000 | tf_op jit(solution)/shard_map/backward/pallas_call | solution.py:502
  125.7 2.5 %collective-permute-start.35 = (bf16[96,4096]{1,0:T(8,128)(2,1)S(1)}, bf16[96,4096]{1,0:T(8,128)(2,1)S(1)}, u32[]{:S(2)}, u32[]{:S(2)}) collective-permute-start(bf16[96,4096]{1,0:T(8,128)(2,1)S(1)} %copy-done), channel_id=1, source_target_pairs={{0,24},{8,16},{16,8},{24,0},{1,25},{9,17},{17,9},{25,1},{2,26},{10... | collective-permute-start | bytes 2359304 | tf_op jit(solution)/shard_map/ppermute | solution.py:539
  132.7 2.8 %collective-permute-start.29 = (bf16[128,512]{1,0:T(8,128)(2,1)S(1)}, bf16[128,512]{1,0:T(8,128)(2,1)S(1)}, u32[]{:S(2)}, u32[]{:S(2)}) collective-permute-start(bf16[128,512]{1,0:T(8,128)(2,1)S(1)} %get-tuple-element.74), channel_id=1, source_target_pairs={{0,6},{1,7},{2,0},{3,1},{4,2},{5,3},{6,4},{7,5},{8,14},{9,15},{10,... | collective-permute-start | bytes 393224 | tf_op jit(solution)/shard_map/ppermute | solution.py:534
  136.7 10.0 %collective-permute-done.35.refs_6_ = bf16[96,4096]{1,0:T(8,128)(2,1)S(1)} collective-permute-done((bf16[96,4096]{1,0:T(8,128)(2,1)S(1)}, bf16[96,4096]{1,0:T(8,128)(2,1)S(1)}, u32[]{:S(2)}, u32[]{:S(2)}) %collective-permute-start.35) | collective-permute-done | bytes 786464 | tf_op jit(solution)/shard_map/ppermute | solution.py:539
  152.4 11.2 %collective-permute-done.36.refs_7_ = bf16[96,4096]{1,0:T(8,128)(2,1)} collective-permute-done((bf16[96,4096]{1,0:T(8,128)(2,1)S(1)}, bf16[96,4096]{1,0:T(8,128)(2,1)}, u32[]{:S(2)}, u32[]{:S(2)}) %collective-permute-start.36) | collective-permute-done | bytes 786464 | tf_op jit(solution)/shard_map/ppermute | solution.py:539
  163.6 3.6 %collective-permute-done.37.refs_8_ = bf16[96,4096]{1,0:T(8,128)(2,1)} collective-permute-done((bf16[96,4096]{1,0:T(8,128)(2,1)S(1)}, bf16[96,4096]{1,0:T(8,128)(2,1)}, u32[]{:S(2)}, u32[]{:S(2)}) %collective-permute-start.37) | collective-permute-done | bytes 786464 | tf_op jit(solution)/shard_map/ppermute | solution.py:539
  167.2 17.9 %collective-permute-done.32.refs_2_ = bf16[96,4096]{1,0:T(8,128)(2,1)} collective-permute-done((bf16[96,4096]{1,0:T(8,128)(2,1)S(1)}, bf16[96,4096]{1,0:T(8,128)(2,1)}, u32[]{:S(2)}, u32[]{:S(2)}) %collective-permute-start.32) | collective-permute-done | bytes 786464 | tf_op jit(solution)/shard_map/ppermute | solution.py:539
  185.0 12.2 %collective-permute-done.33.refs_3_ = bf16[96,4096]{1,0:T(8,128)(2,1)} collective-permute-done((bf16[96,4096]{1,0:T(8,128)(2,1)S(1)}, bf16[96,4096]{1,0:T(8,128)(2,1)}, u32[]{:S(2)}, u32[]{:S(2)}) %collective-permute-start.33) | collective-permute-done | bytes 786464 | tf_op jit(solution)/shard_map/ppermute | solution.py:539
  199.4 14.2 %grads.1 = bf16[3,192,4096]{2,1,0:T(8,128)(2,1)} custom-call(s32[1]{0:T(128)} %bitcast.19.refs_0_, bf16[96,4096]{1,0:T(8,128)(2,1)} %unfold.2.refs_0_.refs_1_, bf16[96,4096]{1,0:T(8,128)(2,1)} %collective-permute-done.32.refs_2_, bf16[96,4096]{1,0:T(8,128)(2,1)} %collective-permute-done.33.refs_3_, bf16[96,4096]{1,0:T(8,128)(2,1)} %collective-permute-done.34.refs_4_, ...), custom_call_target="tpu_custom_call" | custom-call | flops 10000000000 | bytes 15000000 | tf_op jit(solution)/shard_map/grads/pallas_call | solution.py:401
  (129 shorter events, 37.8 us)
Async XLA Ops:
  4.6 11.2 %collective-permute-start.3 = (bf16[128,512]{1,0:T(8,128)(2,1)S(1)}, bf16[128,512]{1,0:T(8,128)(2,1)S(1)}, u32[]{:S(2)}, u32[]{:S(2)}) collective-permute-start(bf16[128,512]{1,0:T(8,128)(2,1)S(1)} %pad_maximum_fusion.refs_2_), channel_id=1, source_target_pairs={{0,4},{1,5},{2,6},{3,7},{4,0},{5,1},{6,2},{7,3},{8,12},{9,13},{10,... | collective-permute-start | bytes 393224 | tf_op jit(solution)/shard_map/ppermute | solution.py:534
  11.4 13.7 %collective-permute-start = (bf16[128,512]{1,0:T(8,128)(2,1)S(1)}, bf16[128,512]{1,0:T(8,128)(2,1)S(1)}, u32[]{:S(2)}, u32[]{:S(2)}) collective-permute-start(bf16[128,512]{1,0:T(8,128)(2,1)S(1)} %pad_maximum_fusion.refs_2_), channel_id=1, source_target_pairs={{0,1},{1,0},{2,3},{3,2},{4,5},{5,4},{6,7},{7,6},{8,9},{9,8},{10,11... | collective-permute-start | bytes 393224 | tf_op jit(solution)/shard_map/ppermute | solution.py:539
  12.2 14.0 %collective-permute-start.2 = (bf16[128,512]{1,0:T(8,128)(2,1)S(1)}, bf16[128,512]{1,0:T(8,128)(2,1)S(1)}, u32[]{:S(2)}, u32[]{:S(2)}) collective-permute-start(bf16[128,512]{1,0:T(8,128)(2,1)S(1)} %collective-permute-done.1.refs_4_), channel_id=1, source_target_pairs={{0,1},{1,0},{2,3},{3,2},{4,5},{5,4},{6,7},{7,6},{8,9},{9,8},{10,11... | collective-permute-start | bytes 393224 | tf_op jit(solution)/shard_map/ppermute | solution.py:539
  15.9 11.9 %collective-permute-start.4 = (bf16[128,512]{1,0:T(8,128)(2,1)S(1)}, bf16[128,512]{1,0:T(8,128)(2,1)S(1)}, u32[]{:S(2)}, u32[]{:S(2)}) collective-permute-start(bf16[128,512]{1,0:T(8,128)(2,1)S(1)} %collective-permute-done.3.refs_6_), channel_id=1, source_target_pairs={{0,1},{1,0},{2,3},{3,2},{4,5},{5,4},{6,7},{7,6},{8,9},{9,8},{10,11... | collective-permute-start | bytes 393224 | tf_op jit(solution)/shard_map/ppermute | solution.py:539
  15.9 14.5 %collective-permute-start.6 = (bf16[128,512]{1,0:T(8,128)(2,1)S(1)}, bf16[128,512]{1,0:T(8,128)(2,1)S(1)}, u32[]{:S(2)}, u32[]{:S(2)}) collective-permute-start(bf16[128,512]{1,0:T(8,128)(2,1)S(1)} %collective-permute-done.5.refs_8_), channel_id=1, source_target_pairs={{0,1},{1,0},{2,3},{3,2},{4,5},{5,4},{6,7},{7,6},{8,9},{9,8},{10,11... | collective-permute-start | bytes 393224 | tf_op jit(solution)/shard_map/ppermute | solution.py:539
  25.1 26.3 %collective-permute-start.16 = (bf16[24,2048]{1,0:T(8,128)(2,1)}, bf16[24,2048]{1,0:T(8,128)(2,1)S(1)}, u32[]{:S(2)}, u32[]{:S(2)}) collective-permute-start(bf16[24,2048]{1,0:T(8,128)(2,1)} %get-tuple-element.50), channel_id=1, source_target_pairs={{0,3},{1,4},{2,5},{3,6},{4,7},{5,0},{6,1},{7,2},{8,11},{9,12},{10,... | collective-permute-start | bytes 294920 | tf_op jit(solution)/shard_map/ppermute | solution.py:534
  25.1 26.4 %collective-permute-start.17 = (bf16[24,2048]{1,0:T(8,128)(2,1)}, bf16[24,2048]{1,0:T(8,128)(2,1)S(1)}, u32[]{:S(2)}, u32[]{:S(2)}) collective-permute-start(bf16[24,2048]{1,0:T(8,128)(2,1)} %get-tuple-element.51), channel_id=1, source_target_pairs={{0,4},{1,5},{2,6},{3,7},{4,0},{5,1},{6,2},{7,3},{8,12},{9,13},{10,... | collective-permute-start | bytes 294920 | tf_op jit(solution)/shard_map/ppermute | solution.py:534
  26.2 25.4 %collective-permute-start.18 = (bf16[24,2048]{1,0:T(8,128)(2,1)}, bf16[24,2048]{1,0:T(8,128)(2,1)S(1)}, u32[]{:S(2)}, u32[]{:S(2)}) collective-permute-start(bf16[24,2048]{1,0:T(8,128)(2,1)} %get-tuple-element.52), channel_id=1, source_target_pairs={{0,5},{1,6},{2,7},{3,0},{4,1},{5,2},{6,3},{7,4},{8,13},{9,14},{10,... | collective-permute-start | bytes 294920 | tf_op jit(solution)/shard_map/ppermute | solution.py:534
  27.8 23.8 %collective-permute-start.19 = (bf16[24,2048]{1,0:T(8,128)(2,1)}, bf16[24,2048]{1,0:T(8,128)(2,1)S(1)}, u32[]{:S(2)}, u32[]{:S(2)}) collective-permute-start(bf16[24,2048]{1,0:T(8,128)(2,1)} %get-tuple-element.53), channel_id=1, source_target_pairs={{0,6},{1,7},{2,0},{3,1},{4,2},{5,3},{6,4},{7,5},{8,14},{9,15},{10,... | collective-permute-start | bytes 294920 | tf_op jit(solution)/shard_map/ppermute | solution.py:534
  30.4 21.3 %collective-permute-start.20 = (bf16[24,2048]{1,0:T(8,128)(2,1)}, bf16[24,2048]{1,0:T(8,128)(2,1)S(1)}, u32[]{:S(2)}, u32[]{:S(2)}) collective-permute-start(bf16[24,2048]{1,0:T(8,128)(2,1)} %get-tuple-element.54), channel_id=1, source_target_pairs={{0,7},{1,0},{2,1},{3,2},{4,3},{5,4},{6,5},{7,6},{8,15},{9,8},{10,9... | collective-permute-start | bytes 294920 | tf_op jit(solution)/shard_map/ppermute | solution.py:534
  54.9 13.1 %collective-permute-start.9 = (bf16[24,2048]{1,0:T(8,128)(2,1)}, bf16[24,2048]{1,0:T(8,128)(2,1)S(1)}, u32[]{:S(2)}, u32[]{:S(2)}) collective-permute-start(bf16[24,2048]{1,0:T(8,128)(2,1)} %get-tuple-element.42), channel_id=1, source_target_pairs={{0,3},{1,4},{2,5},{3,6},{4,7},{5,0},{6,1},{7,2},{8,11},{9,12},{10,... | collective-permute-start | bytes 294920 | tf_op jit(solution)/shard_map/ppermute | solution.py:534
  89.3 16.9 %collective-permute-start.24 = (bf16[24,2048]{1,0:T(8,128)(2,1)}, bf16[24,2048]{1,0:T(8,128)(2,1)S(1)}, u32[]{:S(2)}, u32[]{:S(2)}) collective-permute-start(bf16[24,2048]{1,0:T(8,128)(2,1)} %get-tuple-element.59), channel_id=1, source_target_pairs={{0,4},{1,5},{2,6},{3,7},{4,0},{5,1},{6,2},{7,3},{8,12},{9,13},{10,... | collective-permute-start | bytes 294920 | tf_op jit(solution)/shard_map/ppermute | solution.py:534
  92.0 15.4 %collective-permute-start.25 = (bf16[24,2048]{1,0:T(8,128)(2,1)}, bf16[24,2048]{1,0:T(8,128)(2,1)S(1)}, u32[]{:S(2)}, u32[]{:S(2)}) collective-permute-start(bf16[24,2048]{1,0:T(8,128)(2,1)} %get-tuple-element.60), channel_id=1, source_target_pairs={{0,3},{1,4},{2,5},{3,6},{4,7},{5,0},{6,1},{7,2},{8,11},{9,12},{10,... | collective-permute-start | bytes 294920 | tf_op jit(solution)/shard_map/ppermute | solution.py:534
  92.8 14.6 %collective-permute-start.26 = (bf16[24,2048]{1,0:T(8,128)(2,1)}, bf16[24,2048]{1,0:T(8,128)(2,1)S(1)}, u32[]{:S(2)}, u32[]{:S(2)}) collective-permute-start(bf16[24,2048]{1,0:T(8,128)(2,1)} %get-tuple-element.61), channel_id=1, source_target_pairs={{0,2},{1,3},{2,4},{3,5},{4,6},{5,7},{6,0},{7,1},{8,10},{9,11},{10,... | collective-permute-start | bytes 294920 | tf_op jit(solution)/shard_map/ppermute | solution.py:534
  95.3 12.1 %collective-permute-start.27 = (bf16[24,2048]{1,0:T(8,128)(2,1)}, bf16[24,2048]{1,0:T(8,128)(2,1)S(1)}, u32[]{:S(2)}, u32[]{:S(2)}) collective-permute-start(bf16[24,2048]{1,0:T(8,128)(2,1)} %get-tuple-element.62), channel_id=1, source_target_pairs={{0,1},{1,2},{2,3},{3,4},{4,5},{5,6},{6,7},{7,0},{8,9},{9,10},{10,1... | collective-permute-start | bytes 294920 | tf_op jit(solution)/shard_map/ppermute | solution.py:534
  125.7 20.9 %collective-permute-start.35 = (bf16[96,4096]{1,0:T(8,128)(2,1)S(1)}, bf16[96,4096]{1,0:T(8,128)(2,1)S(1)}, u32[]{:S(2)}, u32[]{:S(2)}) collective-permute-start(bf16[96,4096]{1,0:T(8,128)(2,1)S(1)} %copy-done), channel_id=1, source_target_pairs={{0,24},{8,16},{16,8},{24,0},{1,25},{9,17},{17,9},{25,1},{2,26},{10... | collective-permute-start | bytes 2359304 | tf_op jit(solution)/shard_map/ppermute | solution.py:539
  129.7 18.4 %collective-permute-start.31 = (bf16[128,512]{1,0:T(8,128)(2,1)S(1)}, bf16[128,512]{1,0:T(8,128)(2,1)S(1)}, u32[]{:S(2)}, u32[]{:S(2)}) collective-permute-start(bf16[128,512]{1,0:T(8,128)(2,1)S(1)} %get-tuple-element.75), channel_id=1, source_target_pairs={{0,2},{1,3},{2,4},{3,5},{4,6},{5,7},{6,0},{7,1},{8,10},{9,11},{10,... | collective-permute-start | bytes 393224 | tf_op jit(solution)/shard_map/ppermute | solution.py:534
  130.8 18.8 %collective-permute-start.30 = (bf16[128,512]{1,0:T(8,128)(2,1)S(1)}, bf16[128,512]{1,0:T(8,128)(2,1)S(1)}, u32[]{:S(2)}, u32[]{:S(2)}) collective-permute-start(bf16[128,512]{1,0:T(8,128)(2,1)S(1)} %get-tuple-element.76), channel_id=1, source_target_pairs={{0,4},{1,5},{2,6},{3,7},{4,0},{5,1},{6,2},{7,3},{8,12},{9,13},{10,... | collective-permute-start | bytes 393224 | tf_op jit(solution)/shard_map/ppermute | solution.py:534
  132.7 17.4 %collective-permute-start.29 = (bf16[128,512]{1,0:T(8,128)(2,1)S(1)}, bf16[128,512]{1,0:T(8,128)(2,1)S(1)}, u32[]{:S(2)}, u32[]{:S(2)}) collective-permute-start(bf16[128,512]{1,0:T(8,128)(2,1)S(1)} %get-tuple-element.74), channel_id=1, source_target_pairs={{0,6},{1,7},{2,0},{3,1},{4,2},{5,3},{6,4},{7,5},{8,14},{9,15},{10,... | collective-permute-start | bytes 393224 | tf_op jit(solution)/shard_map/ppermute | solution.py:534
  135.6 28.0 %collective-permute-start.36 = (bf16[96,4096]{1,0:T(8,128)(2,1)S(1)}, bf16[96,4096]{1,0:T(8,128)(2,1)}, u32[]{:S(2)}, u32[]{:S(2)}) collective-permute-start(bf16[96,4096]{1,0:T(8,128)(2,1)S(1)} %copy-done), channel_id=1, source_target_pairs={{0,16},{8,24},{16,0},{24,8},{1,17},{9,25},{17,1},{25,9},{2,18},{10... | collective-permute-start | bytes 2359304 | tf_op jit(solution)/shard_map/ppermute | solution.py:539
  146.6 20.5 %collective-permute-start.37 = (bf16[96,4096]{1,0:T(8,128)(2,1)S(1)}, bf16[96,4096]{1,0:T(8,128)(2,1)}, u32[]{:S(2)}, u32[]{:S(2)}) collective-permute-start(bf16[96,4096]{1,0:T(8,128)(2,1)S(1)} %copy-done), channel_id=1, source_target_pairs={{0,8},{8,0},{16,24},{24,16},{1,9},{9,1},{17,25},{25,17},{2,10},{10... | collective-permute-start | bytes 2359304 | tf_op jit(solution)/shard_map/ppermute | solution.py:539
  148.1 36.9 %collective-permute-start.32 = (bf16[96,4096]{1,0:T(8,128)(2,1)S(1)}, bf16[96,4096]{1,0:T(8,128)(2,1)}, u32[]{:S(2)}, u32[]{:S(2)}) collective-permute-start(bf16[96,4096]{1,0:T(8,128)(2,1)S(1)} %copy-done.2), channel_id=1, source_target_pairs={{0,24},{8,16},{16,8},{24,0},{1,25},{9,17},{17,9},{25,1},{2,26},{10... | collective-permute-start | bytes 2359304 | tf_op jit(solution)/shard_map/ppermute | solution.py:539
  149.6 47.6 %collective-permute-start.33 = (bf16[96,4096]{1,0:T(8,128)(2,1)S(1)}, bf16[96,4096]{1,0:T(8,128)(2,1)}, u32[]{:S(2)}, u32[]{:S(2)}) collective-permute-start(bf16[96,4096]{1,0:T(8,128)(2,1)S(1)} %copy-done.2), channel_id=1, source_target_pairs={{0,16},{8,24},{16,0},{24,8},{1,17},{9,25},{17,1},{25,9},{2,18},{10... | collective-permute-start | bytes 2359304 | tf_op jit(solution)/shard_map/ppermute | solution.py:539
  150.1 49.3 %collective-permute-start.34 = (bf16[96,4096]{1,0:T(8,128)(2,1)S(1)}, bf16[96,4096]{1,0:T(8,128)(2,1)}, u32[]{:S(2)}, u32[]{:S(2)}) collective-permute-start(bf16[96,4096]{1,0:T(8,128)(2,1)S(1)} %copy-done.2), channel_id=1, source_target_pairs={{0,8},{8,0},{16,24},{24,16},{1,9},{9,1},{17,25},{25,17},{2,10},{10... | collective-permute-start | bytes 2359304 | tf_op jit(solution)/shard_map/ppermute | solution.py:539
  (46 other events, 390.6 us)
where the time goes:
time: 214 us
  waiting for transfers between devices  81.5 us (38%)
  Pallas kernels  76.4 us (36%)
  starting transfers between devices  49.6 us (23%)
  local copies, waits for them, and re-layouts  2.8 us (1%)
  other arithmetic  2.39 us (1%)
    ppermute x11, waiting for transfers between devices, flip(): return lax.ppermute(x, axis, [(i, i ^ bit) for i in range(n)])  57 us
    ppermute x27, starting transfers between devices, shift(): return lax.ppermute(x, axis, [(i, (i + k) % n) for i in range(n)])  39.5 us
    ppermute x27, waiting for transfers between devices, shift(): return lax.ppermute(x, axis, [(i, (i + k) % n) for i in range(n)])  24.4 us
    pallas_call x1, Pallas kernels, forward(): pl.pallas_call(lambda *refs: forward_kernel(n, rows, width, *refs), out_s...  20.3 us
    pallas_call x1, Pallas kernels, backward(): pl.pallas_call(lambda *refs: backward_kernel(n, rows, width, *refs), out_...  17.5 us
    pallas_call x1, Pallas kernels, expert_gradients(): pl.pallas_call(lambda *refs: grads_kernel(count, *refs), out_shape=jax.Sh...  14.2 us
    pallas_call x1, Pallas kernels, expert(): pl.pallas_call(lambda *refs: expert_kernel(n, slots, *refs), out_shape=[j...  11 us
    ppermute x11, starting transfers between devices, flip(): return lax.ppermute(x, axis, [(i, i ^ bit) for i in range(n)])  10.1 us
  transfers between devices with their start and end apart: 38, of which 14 were waited for; matrix products, arithmetic and copies ran while one was open for 1% of the time, Pallas kernels for 15%

commit v1 on v0

--- a/solution.py
+++ b/solution.py
@@ -15,7 +15,7 @@
 LOG2E = 1.4426950408889634
 FOLD = 2
 PIECE = FOLD * CAP
-STEP_HEADS = 4
+STEP_HEADS = 8
 F32 = jnp.float32
 BF16 = jnp.bfloat16
 
@@ -47,6 +47,12 @@
 
 
 SMEM_SPEC = pl.BlockSpec(memory_space=pltpu.SMEM)
+
+
+def peer_of(me, b, n, sign):
+    core = me % 2
+    chip = (me // 2 + sign * (b // 2) + n // 2) % (n // 2)
+    return 2 * chip + (core if b % 2 == 0 else 1 - core)
 
 
 def route_kernel(n, rows, width, me_ref, train_ref, ids_ref, gates_ref, up_ref, *outs):
@@ -58,9 +64,7 @@
     hits = jnp.zeros((n, rows), F32)
     level = jnp.zeros((n, rows), F32)
     for k in range(n):
-        j = me + k
-        j = jnp.where(j >= n, j - n, j)
-        same = ids == train_ref[j]
+        same = ids == train_ref[peer_of(me, k, n, 1)]
         hit = jnp.sum(same.astype(F32), axis=0, keepdims=True)
         gate = jnp.sum(jnp.where(same, gates, 0.0), axis=0, keepdims=True)
         hits = jnp.where(row_n == k, hit, hits)
@@ -86,8 +90,10 @@
     for c in range(0, half, chunk):
         picked = mm(first, up_ref[:, c : c + chunk]) + mm(second, up_ref[:, half + c : half + c + chunk])
         picked = (picked * scale).astype(BF16)
-        for k in range(n):
+        for k in range(2):
             blocks[k][:, c : c + chunk] = picked[k * PIECE : (k + 1) * PIECE]
+        for m in range(1, n // 2):
+            blocks[m + 1][:, c : c + chunk] = picked[2 * m * PIECE : 2 * (m + 1) * PIECE]
 
 
 def route(me, trainable, ids, gates, upstream):
@@ -95,7 +101,7 @@
     rows, width = upstream.shape
     half = width // FOLD
     out_shape = [jax.ShapeDtypeStruct((2, n * PIECE, rows), BF16)] + [
-        jax.ShapeDtypeStruct((PIECE, half), BF16) for _ in range(n)
+        jax.ShapeDtypeStruct((PIECE if m < 2 else 2 * PIECE, half), BF16) for m in range(n // 2 + 1)
     ]
     outs = pl.pallas_call(
         lambda *refs: route_kernel(n, rows, width, *refs),
@@ -108,8 +114,10 @@
     return outs[0], list(outs[1:])
 
 
-def unfold_kernel(n, slots, half, *refs):
-    blocks, out_ref = refs[:n], refs[n]
+def unfold(pieces, out_ref):
+    n = len(pieces)
+    slots, width = out_ref.shape
+    half = width // FOLD
     r = iota((slots, n * PIECE), 0)
     s = iota((slots, n * PIECE), 1)
     start = r
@@ -119,22 +127,9 @@
     for f in range(FOLD):
         select = (s == start + f * CAP).astype(BF16)
         for c in range(0, half, chunk):
-            stacked = jnp.concatenate([b[:, c : c + chunk] for b in blocks], axis=0)
+            stacked = jnp.concatenate([ref[at : at + PIECE, c : c + chunk] for ref, at in pieces], axis=0)
             at = f * half + c
             out_ref[:, at : at + chunk] = mm(select, stacked).astype(BF16)
-
-
-def unfold(blocks):
-    n = len(blocks)
-    half = blocks[0].shape[1]
-    slots = n * CAP
-    return pl.pallas_call(
-        lambda *refs: unfold_kernel(n, slots, half, *refs),
-        out_shape=jax.ShapeDtypeStruct((slots, FOLD * half), BF16),
-        compiler_params=params(),
-        cost_estimate=pl.CostEstimate(flops=2 * 10**9, bytes_accessed=10**6, transcendentals=0),
-        name="unfold",
-    )(*blocks)
 
 
 def forward_kernel(n, rows, width, me_ref, span_ref, *refs):
@@ -162,7 +157,7 @@
         mine1 = span_ref[0, 2 * me + 1]
         lane_span = jnp.where(lane_half == 0, mine0, mine1)
         for b in range(n):
-            source = source_of(me, b, n)
+            source = peer_of(me, b, n, -1)
             sub_span = jnp.where(sub_half == 0, span_ref[0, 2 * source], span_ref[0, 2 * source + 1])
             hot = ((sub_span == lane_span) & (lane_in == sub_in - 1)) | (
                 (sub_span > lane_span) & (lane_in == half_rows - 1)
@@ -183,14 +178,21 @@
 
     g = step // (HEADS_PER_GROUP // STEP_HEADS)
     b = b_ref[...]
-    for p in range(STEP_HEADS // 2):
+
+    def paired(p):
         at = p * 2 * HEAD_SIZE
         q0 = q_ref[:, at : at + HEAD_SIZE]
         q1 = q_ref[:, at + HEAD_SIZE : at + 2 * HEAD_SIZE]
-        qb = jnp.concatenate(
+        return jnp.concatenate(
             [jnp.concatenate([q0, b], axis=1), jnp.concatenate([q1, b], axis=1)], axis=0
         )
-        scores = mm_t(ka_ref[g], qb)
+
+    ahead = mm_t(ka_ref[g], paired(0))
+    for p in range(STEP_HEADS // 2):
+        at = p * 2 * HEAD_SIZE
+        scores = ahead
+        if p + 1 < STEP_HEADS // 2:
+            ahead = mm_t(ka_ref[g], paired(p + 1))
         peak = jnp.max(scores, axis=0, keepdims=True)
         exps = jnp.exp2((scores - peak) * (SCALE * LOG2E)).astype(BF16)
         exp_ref[p] = exps
@@ -224,13 +226,6 @@
             picked = picked.astype(BF16)
             for k in range(n):
                 blocks[k][:, i * per_step : (i + 1) * per_step] = picked[k * PIECE : (k + 1) * PIECE]
-
-
-def source_of(me, b, n):
-    core = me % 2
-    chip = me // 2 - b // 2
-    chip = jnp.where(chip < 0, chip + n // 2, chip)
-    return 2 * chip + (core if b % 2 == 0 else 1 - core)
 
 
 def forward(me, span, kv_blocks, query, pick, gain):
@@ -282,30 +277,42 @@
     return grad_gate, grad_up, product
 
 
-def early_kernel(grads_ref, weights, back_ref):
-    back_ref[...] = mm_t(grads_ref[...], weights[0])
-
-
-def early(weighted, weights):
+def early_kernel(n, *refs):
+    blocks, (weights, rows_ref, back_ref) = refs[:n], refs[n:]
+
+    @pl.when(pl.program_id(0) == 0)
+    def _():
+        unfold([(ref, PIECE if b > 2 and b % 2 else 0) for b, ref in enumerate(blocks)], rows_ref)
+
+    back_ref[...] = mm_t(rows_ref[...], weights[0])
+
+
+def early(blocks, weights):
+    n = len(blocks)
     hidden, width = weights.shape[1:]
-    slots = weighted.shape[0]
+    slots = n * CAP
     tile = 256
     return pl.pallas_call(
-        early_kernel,
-        out_shape=jax.ShapeDtypeStruct((slots, hidden), F32),
+        lambda *refs: early_kernel(n, *refs),
+        out_shape=[jax.ShapeDtypeStruct((slots, width), BF16), jax.ShapeDtypeStruct((slots, hidden), F32)],
         grid=(hidden // tile,),
-        in_specs=[whole(weighted.shape), pl.BlockSpec((1, tile, width), lambda i: (2, i, 0))],
-        out_specs=pl.BlockSpec((slots, tile), lambda i: (0, i)),
+        in_specs=[whole(b.shape) for b in blocks] + [pl.BlockSpec((1, tile, width), lambda i: (2, i, 0))],
+        out_specs=[whole((slots, width)), pl.BlockSpec((slots, tile), lambda i: (0, i))],
         compiler_params=params("arbitrary"),
         cost_estimate=pl.CostEstimate(flops=2 * 10**9, bytes_accessed=7 * 10**6, transcendentals=0),
         name="early",
-    )(weighted, weights)
-
-
-def expert_kernel(n, slots, routed_ref, back_ref, weights, *refs):
-    blocks, acc_ref = refs[:n], refs[n]
+    )(*blocks, weights)
+
+
+def expert_kernel(n, slots, *refs):
+    arrived, (back_ref, weights, routed_ref), blocks, acc_ref = refs[:n], refs[n : n + 3], refs[n + 3 : -1], refs[-1]
     step = pl.program_id(0)
     width = acc_ref.shape[1]
+
+    @pl.when(step == 0)
+    def _():
+        unfold([(ref, 0) for ref in arrived], routed_ref)
+
     routed = routed_ref[...]
     gate_in = mm_t(routed, weights[0])
     up_in = mm_t(routed, weights[1])
@@ -340,76 +347,87 @@
                 blocks[k][:, c : c + chunk] = spread[k * PIECE : (k + 1) * PIECE]
 
 
-def expert(routed, back, weights, n):
+def expert(arrived, back, weights):
+    n = len(arrived)
     slots = n * CAP
     hidden, width = weights.shape[1:]
     tile = 256
     half = width // FOLD
-    return list(
-        pl.pallas_call(
-            lambda *refs: expert_kernel(n, slots, *refs),
-            out_shape=[jax.ShapeDtypeStruct((PIECE, half), BF16)] * n,
-            grid=(hidden // tile,),
-            in_specs=[
-                whole(routed.shape),
-                pl.BlockSpec((slots, tile), lambda i: (0, i)),
-                pl.BlockSpec((2, tile, width), lambda i: (0, i, 0)),
-            ],
-            out_specs=[whole((PIECE, half))] * n,
-            scratch_shapes=[pltpu.VMEM((slots, width), F32)],
-            compiler_params=params("arbitrary"),
-            cost_estimate=pl.CostEstimate(flops=8 * 10**9, bytes_accessed=2 * 10**7, transcendentals=0),
-            name="expert",
-        )(routed, back, weights)
-    )
-
-
-def grads_kernel(count, dp_ref, *refs):
+    outs = pl.pallas_call(
+        lambda *refs: expert_kernel(n, slots, *refs),
+        out_shape=[jax.ShapeDtypeStruct((slots, width), BF16)] + [jax.ShapeDtypeStruct((PIECE, half), BF16)] * n,
+        grid=(hidden // tile,),
+        in_specs=[whole(b.shape) for b in arrived]
+        + [
+            pl.BlockSpec((slots, tile), lambda i: (0, i)),
+            pl.BlockSpec((2, tile, width), lambda i: (0, i, 0)),
+        ],
+        out_specs=[whole((slots, width))] + [whole((PIECE, half))] * n,
+        scratch_shapes=[pltpu.VMEM((slots, width), F32)],
+        compiler_params=params("arbitrary"),
+        cost_estimate=pl.CostEstimate(flops=8 * 10**9, bytes_accessed=2 * 10**7, transcendentals=0),
+        name="expert",
+    )(*arrived, back, weights)
+    return outs[0], list(outs[1:])
+
+
+def grads_kernel(count, share, dp_ref, *refs):
     row_parts, grad_parts = refs[:count], refs[count : 2 * count]
-    weights, out_ref, rows_ref, grads_ref, sems = refs[2 * count :]
+    weights, out_ref, rows_ref, grads_ref, w_ref, side_ref, sems = refs[2 * count :]
     part = row_parts[0].shape[0]
+    chunk = out_ref.shape[2]
 
     @pl.when(pl.program_id(0) == 0)
     def _():
+        first = pl.multiple_of(dp_ref[0] * share, 32)
         copies = []
+        for i in range(3):
+            source = weights.at[i, pl.ds(first, share)]
+            copies.append(pltpu.make_async_copy(source, w_ref.at[i], sems.at[2 * count + i]))
+        late = [copies.pop()]
         for i in range(count):
             at = pl.ds(i * part, part)
             copies.append(pltpu.make_async_copy(row_parts[i], rows_ref.at[at], sems.at[i]))
-            copies.append(pltpu.make_async_copy(grad_parts[i], grads_ref.at[at], sems.at[count + i]))
-        for copy in copies:
+            late.append(pltpu.make_async_copy(grad_parts[i], grads_ref.at[at], sems.at[count + i]))
+        for copy in copies + late:
             copy.start()
         for copy in copies:
             copy.wait()
-
-    rows = rows_ref[...]
-    grads = grads_ref[...]
-    gate_in = mm_t(rows, weights[0])
-    up_in = mm_t(rows, weights[1])
-    back = mm_t(grads, weights[2])
-    grad_gate, grad_up, product = gated(gate_in, up_in, back)
-    out_ref[0] = t_mm(grad_gate, rows).astype(BF16)
-    out_ref[1] = t_mm(grad_up, rows).astype(BF16)
-    out_ref[2] = t_mm(product, grads).astype(BF16)
+        rows = rows_ref[...]
+        gate_in = mm_t(rows, w_ref[0])
+        up_in = mm_t(rows, w_ref[1])
+        for copy in late:
+            copy.wait()
+        back = mm_t(grads_ref[...], w_ref[2])
+        for i, side in enumerate(gated(gate_in, up_in, back)):
+            side_ref[i] = side
+
+    at = pl.ds(pl.multiple_of(pl.program_id(0) * chunk, chunk), chunk)
+    out_ref[0] = t_mm(side_ref[0], rows_ref[:, at]).astype(BF16)
+    out_ref[1] = t_mm(side_ref[1], rows_ref[:, at]).astype(BF16)
+    out_ref[2] = t_mm(side_ref[2], grads_ref[:, at]).astype(BF16)
 
 
 def expert_gradients(dp_index, row_parts, grad_parts, weights, share):
     count = len(row_parts)
     width = weights.shape[2]
-    tile = share
-    steps = share // tile
-    part = row_parts[0].shape
+    slots = row_parts[0].shape[0]
+    total = count * slots
+    chunk = width // 4
+    anywhere = pl.BlockSpec(memory_space=pl.ANY)
     return pl.pallas_call(
-        lambda *refs: grads_kernel(count, *refs),
+        lambda *refs: grads_kernel(count, share, *refs),
         out_shape=jax.ShapeDtypeStruct((3, share, width), BF16),
-        grid_spec=pltpu.PrefetchScalarGridSpec(
-            num_scalar_prefetch=1,
-            grid=(steps,),
-            in_specs=[pl.BlockSpec(memory_space=pl.ANY)] * (2 * count)
-            + [pl.BlockSpec((3, tile, width), lambda i, d: (0, d[0] * steps + i, 0))],
-            out_specs=pl.BlockSpec((3, tile, width), lambda i, d: (0, i, 0)),
-            scratch_shapes=[pltpu.VMEM((count * part[0], width), BF16)] * 2
-            + [pltpu.SemaphoreType.DMA((2 * count,))],
-        ),
+        grid=(width // chunk,),
+        in_specs=[SMEM_SPEC] + [anywhere] * (2 * count + 1),
+        out_specs=pl.BlockSpec((3, share, chunk), lambda i: (0, 0, i)),
+        scratch_shapes=[
+            pltpu.VMEM((total, width), BF16),
+            pltpu.VMEM((total, width), BF16),
+            pltpu.VMEM((3, share, width), BF16),
+            pltpu.VMEM((3, total, share), BF16),
+            pltpu.SemaphoreType.DMA((2 * count + 3,)),
+        ],
         compiler_params=params("arbitrary"),
         cost_estimate=pl.CostEstimate(flops=10**10, bytes_accessed=15 * 10**6, transcendentals=0),
         name="grads",
@@ -454,15 +472,21 @@
     grad_all = gm_ref[step].astype(F32) * inv_ref[...]
     grad_b = grad_all.astype(BF16)
     prod = (grad_b.astype(F32) * mixed_ref[:, pl.ds(col, per_step)].astype(F32)).astype(BF16)
+
+    def stack(x, p):
+        at = p * 2 * HEAD_SIZE
+        return jnp.concatenate([x[:, at : at + HEAD_SIZE], x[:, at + HEAD_SIZE : at + 2 * HEAD_SIZE]], axis=0)
+
+    def push(p):
+        return mm_t(va_ref[g], jnp.concatenate([stack(grad_b, p), stack(prod, p)], axis=1))
+
+    ahead = push(0)
     for p in range(STEP_HEADS // 2):
         at = p * 2 * HEAD_SIZE
-
-        def stack(x):
-            return jnp.concatenate([x[:, at : at + HEAD_SIZE], x[:, at + HEAD_SIZE : at + 2 * HEAD_SIZE]], axis=0)
-
-        gs = stack(grad_b)
-        gb = jnp.concatenate([gs, stack(prod)], axis=1)
-        pushed = mm_t(va_ref[g], gb)
+        gs = stack(grad_b, p)
+        pushed = ahead
+        if p + 1 < STEP_HEADS // 2:
+            ahead = push(p + 1)
         exps = exp_ref[p]
         slopes = (exps.astype(F32) * pushed).astype(BF16)
         qs = jnp.concatenate([q_ref[:, at : at + HEAD_SIZE], q_ref[:, at + HEAD_SIZE : at + 2 * HEAD_SIZE]], axis=0)
@@ -539,15 +563,12 @@
     return lax.ppermute(x, axis, [(i, i ^ bit) for i in range(n)])
 
 
-def far_first(n):
-    return sorted(range(1, n), key=lambda k: -min(k, n - k))
-
-
 def exchange(blocks, sign):
     n = len(blocks)
     got = [blocks[0]] + [None] * (n - 1)
-    for k in far_first(n):
-        got[k] = shift(blocks[k], "ctx", sign * k)
+    chips = n // 2
+    for b in sorted(range(1, n), key=lambda b: -min(b // 2, chips - b // 2)):
+        got[b] = lax.ppermute(blocks[b], "ctx", [(i, peer_of(i, b, n, sign)) for i in range(n)])
     return got
 
 
@@ -583,16 +604,17 @@
         kv_blocks += [block, flip(block, "ctx", 1)]
 
     pick, grad_blocks = route(me, trainable, expert_ids[0].T, expert_gates[0].T, grad_out)
-    grad_blocks = exchange(grad_blocks, 1)
-    weighted = unfold(grad_blocks)
+    pairs = [shift(grad_blocks[m + 1], "ctx", 2 * m) for m in range(1, chips)]
+    grad_blocks = [grad_blocks[0], flip(grad_blocks[1], "ctx", 1)]
+    for pair in pairs:
+        grad_blocks += [pair, flip(pair, "ctx", 1)]
+    weighted, back_rows = early(grad_blocks, weights)
     all_weighted = gather_docs(weighted)
-    back_rows = early(weighted, weights)
 
     fwd, row_blocks = forward(me, span_order, kv_blocks, query[0], pick, gain)
     row_blocks = exchange(row_blocks, 1)
-    routed = unfold(row_blocks)
+    routed, returned = expert(row_blocks, back_rows, weights)
     all_routed = gather_docs(routed)
-    returned = expert(routed, back_rows, weights, n)
     back = exchange(returned, -1)
     share = weights.shape[1] // lax.axis_size("dp")
     expert_grads = expert_gradients(dp_index, all_routed, all_weighted, weights, share)

time: 214 us -> 205 us (0.958)
  Pallas kernels: 76.4 us -> 61.6 us
  waiting for transfers between devices: 81.5 us -> 87.5 us
    ppermute x27 -> x9, starting transfers between devices: 39.5 us -> 16.2 us  [shift(): return lax.ppermute(x, axis, [(i, (i + k) % n) for i in range(n)])]
    ppermute x0 -> x14, starting transfers between devices: none -> 20.3 us  [exchange(): lax.ppermute(blocks[b], 'ctx', [(i, peer_of(i, b, n, sign)) for i in rang...]
    ppermute x0 -> x14, waiting for transfers between devices: none -> 16.9 us  [exchange(): lax.ppermute(blocks[b], 'ctx', [(i, peer_of(i, b, n, sign)) for i in rang...]
    ppermute x11 -> x15, waiting for transfers between devices: 57 us -> 48.6 us  [flip(): return lax.ppermute(x, axis, [(i, i ^ bit) for i in range(n)])]
    pallas_call x4 -> x2, Pallas kernels: 24.9 us -> 18 us  [the longest x1 11.8 us: expert_gradients(): pl.pallas_call(lambda *refs: grads_kernel(count, share, *refs), out_shape...]
    pallas_call x1, Pallas kernels: 20.3 us -> 14.1 us  [forward(): pl.pallas_call(lambda *refs: forward_kernel(n, rows, width, *refs), out_s...]
    ppermute x27 -> x9, waiting for transfers between devices: 24.4 us -> 22 us  [shift(): return lax.ppermute(x, axis, [(i, (i + k) % n) for i in range(n)])]
    pallas_call x1, Pallas kernels: 17.5 us -> 15.1 us  [backward(): pl.pallas_call(lambda *refs: backward_kernel(n, rows, width, *refs), out_...]
  transfers between devices with their start and end apart: 38 -> 38, of which waited for: 14 -> 13; matrix products, arithmetic and copies ran while one was open for 1% -> 1% of each run, Pallas kernels for 15% -> 11%
where the time goes in v1:
time: 205 us
  waiting for transfers between devices  87.5 us (43%)
  Pallas kernels  61.6 us (30%)
  starting transfers between devices  48.8 us (24%)
  local copies, waits for them, and re-layouts  3.58 us (2%)
  other arithmetic  2.39 us (1%)
    ppermute x15, waiting for transfers between devices, flip(): return lax.ppermute(x, axis, [(i, i ^ bit) for i in range(n)])  48.6 us
    ppermute x9, waiting for transfers between devices, shift(): return lax.ppermute(x, axis, [(i, (i + k) % n) for i in range(n)])  22 us
    ppermute x14, starting transfers between devices, exchange(): lax.ppermute(blocks[b], 'ctx', [(i, peer_of(i, b, n, sign)) for i in rang...  20.3 us
    ppermute x14, waiting for transfers between devices, exchange(): lax.ppermute(blocks[b], 'ctx', [(i, peer_of(i, b, n, sign)) for i in rang...  16.9 us
    ppermute x9, starting transfers between devices, shift(): return lax.ppermute(x, axis, [(i, (i + k) % n) for i in range(n)])  16.2 us
    pallas_call x1, Pallas kernels, backward(): pl.pallas_call(lambda *refs: backward_kernel(n, rows, width, *refs), out_...  15.1 us
    pallas_call x1, Pallas kernels, forward(): pl.pallas_call(lambda *refs: forward_kernel(n, rows, width, *refs), out_s...  14.1 us
    ppermute x15, starting transfers between devices, flip(): return lax.ppermute(x, axis, [(i, i ^ bit) for i in range(n)])  12.2 us
  transfers between devices with their start and end apart: 38, of which 13 were waited for; matrix products, arithmetic and copies ran while one was open for 1% of the time, Pallas kernels for 11%

profile of v1, /device:TPU:0, one launch (start us, length us, event | category | flops | bytes accessed | tf_op | source)
XLA Modules:
  0.0 205.0 jit_solution(1455721864320473271)
XLA Ops:
  2.1 2.6 %collective-permute-start.1 = (bf16[128,512]{1,0:T(8,128)(2,1)S(1)}, bf16[128,512]{1,0:T(8,128)(2,1)S(1)}, u32[]{:S(2)}, u32[]{:S(2)}) collective-permute-start(bf16[128,512]{1,0:T(8,128)(2,1)S(1)} %pad_maximum_fusion.refs_2_), channel_id=1, source_target_pairs={{0,2},{1,3},{2,4},{3,5},{4,6},{5,7},{6,0},{7,1},{8,10},{9,11},{10,... | collective-permute-start | bytes 393224 | tf_op jit(solution)/shard_map/ppermute | solution.py:558
  4.7 2.8 %route.1 = (bf16[2,192,128]{2,1,0:T(8,128)(2,1)}, bf16[24,2048]{1,0:T(8,128)(2,1)}, bf16[24,2048]{1,0:T(8,128)(2,1)}, bf16[48,2048]{1,0:T(8,128)(2,1)}, bf16[48,...) custom-call(s32[1]{0:T(128)} %bitcast.refs_0_, s32[8]{0:T(128)} %refs_1_.2, s32[8,128]{1,0:T(8,128)} %bitcast.51, ...), custom_call_target="tpu_custom_call" | custom-call | flops 4000000000 | bytes 2000000 | tf_op jit(solution)/shard_map/route/pallas_call | solution.py:106
  10.1 2.9 %collective-permute-start.5 = (bf16[128,512]{1,0:T(8,128)(2,1)S(1)}, bf16[128,512]{1,0:T(8,128)(2,1)S(1)}, u32[]{:S(2)}, u32[]{:S(2)}) collective-permute-start(bf16[128,512]{1,0:T(8,128)(2,1)S(1)} %pad_maximum_fusion.refs_2_), channel_id=1, source_target_pairs={{0,6},{1,7},{2,0},{3,1},{4,2},{5,3},{6,4},{7,5},{8,14},{9,15},{10,... | collective-permute-start | bytes 393224 | tf_op jit(solution)/shard_map/ppermute | solution.py:558
  14.5 8.6 %collective-permute-done.3.refs_6_ = bf16[128,512]{1,0:T(8,128)(2,1)S(1)} collective-permute-done((bf16[128,512]{1,0:T(8,128)(2,1)S(1)}, bf16[128,512]{1,0:T(8,128)(2,1)S(1)}, u32[]{:S(2)}, u32[]{:S(2)}) %collective-permute-start.3) | collective-permute-done | bytes 131104 | tf_op jit(solution)/shard_map/ppermute | solution.py:558
  23.7 9.8 %collective-permute-done.17.refs_4_ = bf16[48,2048]{1,0:T(8,128)(2,1)S(1)} collective-permute-done((bf16[48,2048]{1,0:T(8,128)(2,1)}, bf16[48,2048]{1,0:T(8,128)(2,1)S(1)}, u32[]{:S(2)}, u32[]{:S(2)}) %collective-permute-start.17) | collective-permute-done | bytes 196640 | tf_op jit(solution)/shard_map/ppermute | solution.py:558
  35.2 14.1 %forward.1 = (bf16[2,1024,256]{2,1,0:T(8,128)(2,1)}, bf16[2,1024,256]{2,1,0:T(8,128)(2,1)}, bf16[2,128,1024]{2,1,0:T(8,128)(2,1)}, bf16[2,144,1024]{2,1,0:T(8,12...) custom-call(s32[1]{0:T(128)} %bitcast.refs_0_, ...), custom_call_target="tpu_custom_call" | custom-call | flops 10000000000 | bytes 20000000 | tf_op jit(solution)/shard_map/forward/pallas_call | solution.py:255
  49.5 4.6 %collective-permute-start.8 = (bf16[24,2048]{1,0:T(8,128)(2,1)}, bf16[24,2048]{1,0:T(8,128)(2,1)S(1)}, u32[]{:S(2)}, u32[]{:S(2)}) collective-permute-start(bf16[24,2048]{1,0:T(8,128)(2,1)} %get-tuple-element.41), channel_id=1, source_target_pairs={{0,2},{1,3},{2,4},{3,5},{4,6},{5,7},{6,0},{7,1},{8,10},{9,11},{10,... | collective-permute-start | bytes 294920 | tf_op jit(solution)/shard_map/ppermute | solution.py:571
  55.2 3.6 %collective-permute-done.8.refs_2_ = bf16[24,2048]{1,0:T(8,128)(2,1)S(1)} collective-permute-done((bf16[24,2048]{1,0:T(8,128)(2,1)}, bf16[24,2048]{1,0:T(8,128)(2,1)S(1)}, u32[]{:S(2)}, u32[]{:S(2)}) %collective-permute-start.8) | collective-permute-done | bytes 98336 | tf_op jit(solution)/shard_map/ppermute | solution.py:571
  63.9 6.2 %early.1 = (bf16[96,4096]{1,0:T(8,128)(2,1)}, f32[96,768]{1,0:T(8,128)}) custom-call(bf16[24,2048]{1,0:T(8,128)(2,1)} %get-tuple-element.47.refs_0_, bf16[24,2048]{1,0:T(8,128)(2,1)} %copy-done.7, bf16[48,2048]{1,0:T(8,128)(2,1)} %copy-done, bf16[48,2048]{1,0:T(8,128)(2,1)} %copy-done.3, bf16[48,2048]{1,0:T(8,128)(2,1)} %copy-done.1, ...), custom_call_target="tpu_custom_call" | custom-call | flops 2000000000 | bytes 7000000 | tf_op jit(solution)/shard_map/early/pallas_call | solution.py:295
  72.0 11.6 %expert.1 = (bf16[96,4096]{1,0:T(8,128)(2,1)}, bf16[24,2048]{1,0:T(8,128)(2,1)}, bf16[24,2048]{1,0:T(8,128)(2,1)}, bf16[24,2048]{1,0:T(8,128)(2,1)}, bf16[24,204...) custom-call(bf16[24,2048]{1,0:T(8,128)(2,1)} %get-tuple-element.39.r, ...), custom_call_target="tpu_custom_call" | custom-call | flops 8000000000 | bytes 20000000 | tf_op jit(solution)/shard_map/expert/pallas_call | solution.py:356
  83.9 4.6 %collective-permute-start.22 = (bf16[24,2048]{1,0:T(8,128)(2,1)}, bf16[24,2048]{1,0:T(8,128)(2,1)S(1)}, u32[]{:S(2)}, u32[]{:S(2)}) collective-permute-start(bf16[24,2048]{1,0:T(8,128)(2,1)} %get-tuple-element.55), channel_id=1, source_target_pairs={{0,6},{1,7},{2,0},{3,1},{4,2},{5,3},{6,4},{7,5},{8,14},{9,15},{10,... | collective-permute-start | bytes 294920 | tf_op jit(solution)/shard_map/ppermute | solution.py:571
  88.5 2.4 %collective-permute-start.25 = (bf16[24,2048]{1,0:T(8,128)(2,1)}, bf16[24,2048]{1,0:T(8,128)(2,1)S(1)}, u32[]{:S(2)}, u32[]{:S(2)}) collective-permute-start(bf16[24,2048]{1,0:T(8,128)(2,1)} %get-tuple-element.58), channel_id=1, source_target_pairs={{0,5},{1,4},{2,7},{3,6},{4,1},{5,0},{6,3},{7,2},{8,13},{9,12},{10,... | collective-permute-start | bytes 294920 | tf_op jit(solution)/shard_map/ppermute | solution.py:571
  90.9 2.0 collective-permute-start.26
  94.3 10.6 %collective-permute-done.24.refs_4_ = bf16[24,2048]{1,0:T(8,128)(2,1)S(1)} collective-permute-done((bf16[24,2048]{1,0:T(8,128)(2,1)}, bf16[24,2048]{1,0:T(8,128)(2,1)S(1)}, u32[]{:S(2)}, u32[]{:S(2)}) %collective-permute-start.24) | collective-permute-done | bytes 98336 | tf_op jit(solution)/shard_map/ppermute | solution.py:571
  105.8 15.1 %backward.1 = (bf16[128,4096]{1,0:T(8,128)(2,1)}, f32[4,128,512]{2,1,0:T(8,128)}, bf16[4,128,512]{2,1,0:T(8,128)(2,1)}) custom-call(bf16[24,2048]{1,0:T(8,128)(2,1)} %get-tuple-element.53.refs_0_, bf16[24,2048]{1,0:T(8,128)(2,1)} %copy-done.22, bf16[24,2048]{1,0:T(8,128)(2,1)} %copy-done.23, bf16[24,2048]{1,0:T(8,128)(2,1)} %copy-done.25, ...), custom_call_target="tpu_custom_call" | custom-call | flops 20000000000 | bytes 20000000 | tf_op jit(solution)/shard_map/backward/pallas_call | solution.py:526
  121.8 2.5 %collective-permute-start.32 = (bf16[96,4096]{1,0:T(8,128)(2,1)S(1)}, bf16[96,4096]{1,0:T(8,128)(2,1)S(1)}, u32[]{:S(2)}, u32[]{:S(2)}) collective-permute-start(bf16[96,4096]{1,0:T(8,128)(2,1)S(1)} %copy-done.9), channel_id=1, source_target_pairs={{0,24},{8,16},{16,8},{24,0},{1,25},{9,17},{17,9},{25,1},{2,26},{10... | collective-permute-start | bytes 2359304 | tf_op jit(solution)/shard_map/ppermute | solution.py:563
  125.7 1.9 collective-permute-start.31
  129.5 2.8 %collective-permute-start.29 = (bf16[128,512]{1,0:T(8,128)(2,1)S(1)}, bf16[128,512]{1,0:T(8,128)(2,1)S(1)}, u32[]{:S(2)}, u32[]{:S(2)}) collective-permute-start(bf16[128,512]{1,0:T(8,128)(2,1)S(1)} %get-tuple-element.74), channel_id=1, source_target_pairs={{0,6},{1,7},{2,0},{3,1},{4,2},{5,3},{6,4},{7,5},{8,14},{9,15},{10,... | collective-permute-start | bytes 393224 | tf_op jit(solution)/shard_map/ppermute | solution.py:558
  134.9 3.6 %collective-permute-done.30 = bf16[128,512]{1,0:T(8,128)(2,1)S(1)} collective-permute-done((bf16[128,512]{1,0:T(8,128)(2,1)S(1)}, bf16[128,512]{1,0:T(8,128)(2,1)S(1)}, u32[]{:S(2)}, u32[]{:S(2)}) %collective-permute-start.30) | collective-permute-done | bytes 131104 | tf_op jit(solution)/shard_map/ppermute | solution.py:558
  138.5 2.3 %collective-permute-start.35 = (bf16[96,4096]{1,0:T(8,128)(2,1)S(1)}, bf16[96,4096]{1,0:T(8,128)(2,1)}, u32[]{:S(2)}, u32[]{:S(2)}) collective-permute-start(bf16[96,4096]{1,0:T(8,128)(2,1)S(1)} %copy-done.8), channel_id=1, source_target_pairs={{0,24},{8,16},{16,8},{24,0},{1,25},{9,17},{17,9},{25,1},{2,26},{10... | collective-permute-start | bytes 2359304 | tf_op jit(solution)/shard_map/ppermute | solution.py:563
  146.3 13.9 %collective-permute-done.33.refs_3_ = bf16[96,4096]{1,0:T(8,128)(2,1)} collective-permute-done((bf16[96,4096]{1,0:T(8,128)(2,1)S(1)}, bf16[96,4096]{1,0:T(8,128)(2,1)}, u32[]{:S(2)}, u32[]{:S(2)}) %collective-permute-start.33) | collective-permute-done | bytes 786464 | tf_op jit(solution)/shard_map/ppermute | solution.py:563
  160.2 16.8 %collective-permute-done.35.refs_6_ = bf16[96,4096]{1,0:T(8,128)(2,1)} collective-permute-done((bf16[96,4096]{1,0:T(8,128)(2,1)S(1)}, bf16[96,4096]{1,0:T(8,128)(2,1)}, u32[]{:S(2)}, u32[]{:S(2)}) %collective-permute-start.35) | collective-permute-done | bytes 786464 | tf_op jit(solution)/shard_map/ppermute | solution.py:563
  177.0 15.9 %collective-permute-done.36.refs_7_ = bf16[96,4096]{1,0:T(8,128)(2,1)} collective-permute-done((bf16[96,4096]{1,0:T(8,128)(2,1)S(1)}, bf16[96,4096]{1,0:T(8,128)(2,1)}, u32[]{:S(2)}, u32[]{:S(2)}) %collective-permute-start.36) | collective-permute-done | bytes 786464 | tf_op jit(solution)/shard_map/ppermute | solution.py:563
  193.0 11.8 %grads.1 = bf16[3,192,4096]{2,1,0:T(8,128)(2,1)} custom-call(s32[1]{0:T(128)} %bitcast.19.refs_0_, bf16[96,4096]{1,0:T(8,128)(2,1)} %get-tuple-element.70.refs_1_, bf16[96,4096]{1,0:T(8,128)(2,1)} %copy-done.10, bf16[96,4096]{1,0:T(8,128)(2,1)} %collective-permute-done.33.refs_3_, bf16[96,4096]{1,0:T(8,128)(2,1)} %collective-permute-done.34.refs_4_, ...), custom_call_target="tpu_custom_call" | custom-call | flops 10000000000 | bytes 15000000 | tf_op jit(solution)/shard_map/grads/pallas_call | solution.py:418
  (127 shorter events, 30.9 us)
Async XLA Ops:
  1.5 11.5 %collective-permute-start = (bf16[128,512]{1,0:T(8,128)(2,1)S(1)}, bf16[128,512]{1,0:T(8,128)(2,1)S(1)}, u32[]{:S(2)}, u32[]{:S(2)}) collective-permute-start(bf16[128,512]{1,0:T(8,128)(2,1)S(1)} %pad_maximum_fusion.refs_2_), channel_id=1, source_target_pairs={{0,1},{1,0},{2,3},{3,2},{4,5},{5,4},{6,7},{7,6},{8,9},{9,8},{10,11... | collective-permute-start | bytes 393224 | tf_op jit(solution)/shard_map/ppermute | solution.py:563
  2.1 11.3 %collective-permute-start.1 = (bf16[128,512]{1,0:T(8,128)(2,1)S(1)}, bf16[128,512]{1,0:T(8,128)(2,1)S(1)}, u32[]{:S(2)}, u32[]{:S(2)}) collective-permute-start(bf16[128,512]{1,0:T(8,128)(2,1)S(1)} %pad_maximum_fusion.refs_2_), channel_id=1, source_target_pairs={{0,2},{1,3},{2,4},{3,5},{4,6},{5,7},{6,0},{7,1},{8,10},{9,11},{10,... | collective-permute-start | bytes 393224 | tf_op jit(solution)/shard_map/ppermute | solution.py:558
  7.5 16.1 %collective-permute-start.15 = (bf16[48,2048]{1,0:T(8,128)(2,1)}, bf16[48,2048]{1,0:T(8,128)(2,1)S(1)}, u32[]{:S(2)}, u32[]{:S(2)}) collective-permute-start(bf16[48,2048]{1,0:T(8,128)(2,1)} %get-tuple-element.49), channel_id=1, source_target_pairs={{0,2},{1,3},{2,4},{3,5},{4,6},{5,7},{6,0},{7,1},{8,10},{9,11},{10,... | collective-permute-start | bytes 589832 | tf_op jit(solution)/shard_map/ppermute | solution.py:558
  9.1 14.0 %collective-permute-start.3 = (bf16[128,512]{1,0:T(8,128)(2,1)S(1)}, bf16[128,512]{1,0:T(8,128)(2,1)S(1)}, u32[]{:S(2)}, u32[]{:S(2)}) collective-permute-start(bf16[128,512]{1,0:T(8,128)(2,1)S(1)} %pad_maximum_fusion.refs_2_), channel_id=1, source_target_pairs={{0,4},{1,5},{2,6},{3,7},{4,0},{5,1},{6,2},{7,3},{8,12},{9,13},{10,... | collective-permute-start | bytes 393224 | tf_op jit(solution)/shard_map/ppermute | solution.py:558
  10.1 13.0 %collective-permute-start.5 = (bf16[128,512]{1,0:T(8,128)(2,1)S(1)}, bf16[128,512]{1,0:T(8,128)(2,1)S(1)}, u32[]{:S(2)}, u32[]{:S(2)}) collective-permute-start(bf16[128,512]{1,0:T(8,128)(2,1)S(1)} %pad_maximum_fusion.refs_2_), channel_id=1, source_target_pairs={{0,6},{1,7},{2,0},{3,1},{4,2},{5,3},{6,4},{7,5},{8,14},{9,15},{10,... | collective-permute-start | bytes 393224 | tf_op jit(solution)/shard_map/ppermute | solution.py:558
  13.0 20.5 %collective-permute-start.17 = (bf16[48,2048]{1,0:T(8,128)(2,1)}, bf16[48,2048]{1,0:T(8,128)(2,1)S(1)}, u32[]{:S(2)}, u32[]{:S(2)}) collective-permute-start(bf16[48,2048]{1,0:T(8,128)(2,1)} %get-tuple-element.50), channel_id=1, source_target_pairs={{0,4},{1,5},{2,6},{3,7},{4,0},{5,1},{6,2},{7,3},{8,12},{9,13},{10,... | collective-permute-start | bytes 589832 | tf_op jit(solution)/shard_map/ppermute | solution.py:558
  13.4 20.2 %collective-permute-start.19 = (bf16[48,2048]{1,0:T(8,128)(2,1)}, bf16[48,2048]{1,0:T(8,128)(2,1)S(1)}, u32[]{:S(2)}, u32[]{:S(2)}) collective-permute-start(bf16[48,2048]{1,0:T(8,128)(2,1)} %get-tuple-element.51), channel_id=1, source_target_pairs={{0,6},{1,7},{2,0},{3,1},{4,2},{5,3},{6,4},{7,5},{8,14},{9,15},{10,... | collective-permute-start | bytes 589832 | tf_op jit(solution)/shard_map/ppermute | solution.py:558
  33.5 16.0 %collective-permute-start.14 = (bf16[24,2048]{1,0:T(8,128)(2,1)}, bf16[24,2048]{1,0:T(8,128)(2,1)S(1)}, u32[]{:S(2)}, u32[]{:S(2)}) collective-permute-start(bf16[24,2048]{1,0:T(8,128)(2,1)} %get-tuple-element.48), channel_id=1, source_target_pairs={{0,1},{1,0},{2,3},{3,2},{4,5},{5,4},{6,7},{7,6},{8,9},{9,8},{10,11... | collective-permute-start | bytes 294920 | tf_op jit(solution)/shard_map/ppermute | solution.py:563
  33.5 25.8 %collective-permute-start.16 = (bf16[48,2048]{1,0:T(8,128)(2,1)S(1)}, bf16[48,2048]{1,0:T(8,128)(2,1)S(1)}, u32[]{:S(2)}, u32[]{:S(2)}) collective-permute-start(bf16[48,2048]{1,0:T(8,128)(2,1)S(1)} %collective-permute-done.15.refs_2_), channel_id=1, source_target_pairs={{0,1},{1,0},{2,3},{3,2},{4,5},{5,4},{6,7},{7,6},{8,9},{9,8},{10,11... | collective-permute-start | bytes 589832 | tf_op jit(solution)/shard_map/ppermute | solution.py:563
  34.0 26.9 %collective-permute-start.18 = (bf16[48,2048]{1,0:T(8,128)(2,1)S(1)}, bf16[48,2048]{1,0:T(8,128)(2,1)S(1)}, u32[]{:S(2)}, u32[]{:S(2)}) collective-permute-start(bf16[48,2048]{1,0:T(8,128)(2,1)S(1)} %collective-permute-done.17.refs_4_), channel_id=1, source_target_pairs={{0,1},{1,0},{2,3},{3,2},{4,5},{5,4},{6,7},{7,6},{8,9},{9,8},{10,11... | collective-permute-start | bytes 589832 | tf_op jit(solution)/shard_map/ppermute | solution.py:563
  34.1 28.3 %collective-permute-start.20 = (bf16[48,2048]{1,0:T(8,128)(2,1)S(1)}, bf16[48,2048]{1,0:T(8,128)(2,1)S(1)}, u32[]{:S(2)}, u32[]{:S(2)}) collective-permute-start(bf16[48,2048]{1,0:T(8,128)(2,1)S(1)} %collective-permute-done.19.refs_6_), channel_id=1, source_target_pairs={{0,1},{1,0},{2,3},{3,2},{4,5},{5,4},{6,7},{7,6},{8,9},{9,8},{10,11... | collective-permute-start | bytes 589832 | tf_op jit(solution)/shard_map/ppermute | solution.py:563
  54.1 15.9 %collective-permute-start.9 = (bf16[24,2048]{1,0:T(8,128)(2,1)}, bf16[24,2048]{1,0:T(8,128)(2,1)S(1)}, u32[]{:S(2)}, u32[]{:S(2)}) collective-permute-start(bf16[24,2048]{1,0:T(8,128)(2,1)} %get-tuple-element.42), channel_id=1, source_target_pairs={{0,3},{1,2},{2,5},{3,4},{4,7},{5,6},{6,1},{7,0},{8,11},{9,10},{10,... | collective-permute-start | bytes 294920 | tf_op jit(solution)/shard_map/ppermute | solution.py:571
  58.8 11.2 %collective-permute-start.10 = (bf16[24,2048]{1,0:T(8,128)(2,1)}, bf16[24,2048]{1,0:T(8,128)(2,1)S(1)}, u32[]{:S(2)}, u32[]{:S(2)}) collective-permute-start(bf16[24,2048]{1,0:T(8,128)(2,1)} %get-tuple-element.43), channel_id=1, source_target_pairs={{0,4},{1,5},{2,6},{3,7},{4,0},{5,1},{6,2},{7,3},{8,12},{9,13},{10,... | collective-permute-start | bytes 294920 | tf_op jit(solution)/shard_map/ppermute | solution.py:571
  88.5 16.4 %collective-permute-start.24 = (bf16[24,2048]{1,0:T(8,128)(2,1)}, bf16[24,2048]{1,0:T(8,128)(2,1)S(1)}, u32[]{:S(2)}, u32[]{:S(2)}) collective-permute-start(bf16[24,2048]{1,0:T(8,128)(2,1)} %get-tuple-element.57), channel_id=1, source_target_pairs={{0,4},{1,5},{2,6},{3,7},{4,0},{5,1},{6,2},{7,3},{8,12},{9,13},{10,... | collective-permute-start | bytes 294920 | tf_op jit(solution)/shard_map/ppermute | solution.py:571
  88.5 16.7 %collective-permute-start.25 = (bf16[24,2048]{1,0:T(8,128)(2,1)}, bf16[24,2048]{1,0:T(8,128)(2,1)S(1)}, u32[]{:S(2)}, u32[]{:S(2)}) collective-permute-start(bf16[24,2048]{1,0:T(8,128)(2,1)} %get-tuple-element.58), channel_id=1, source_target_pairs={{0,5},{1,4},{2,7},{3,6},{4,1},{5,0},{6,3},{7,2},{8,13},{9,12},{10,... | collective-permute-start | bytes 294920 | tf_op jit(solution)/shard_map/ppermute | solution.py:571
  90.9 14.3 %collective-permute-start.26 = (bf16[24,2048]{1,0:T(8,128)(2,1)}, bf16[24,2048]{1,0:T(8,128)(2,1)S(1)}, u32[]{:S(2)}, u32[]{:S(2)}) collective-permute-start(bf16[24,2048]{1,0:T(8,128)(2,1)} %get-tuple-element.59), channel_id=1, source_target_pairs={{0,2},{1,3},{2,4},{3,5},{4,6},{5,7},{6,0},{7,1},{8,10},{9,11},{10,... | collective-permute-start | bytes 294920 | tf_op jit(solution)/shard_map/ppermute | solution.py:571
  92.9 12.3 %collective-permute-start.27 = (bf16[24,2048]{1,0:T(8,128)(2,1)}, bf16[24,2048]{1,0:T(8,128)(2,1)S(1)}, u32[]{:S(2)}, u32[]{:S(2)}) collective-permute-start(bf16[24,2048]{1,0:T(8,128)(2,1)} %get-tuple-element.60), channel_id=1, source_target_pairs={{0,3},{1,2},{2,5},{3,4},{4,7},{5,6},{6,1},{7,0},{8,11},{9,10},{10,... | collective-permute-start | bytes 294920 | tf_op jit(solution)/shard_map/ppermute | solution.py:571
  121.8 21.4 %collective-permute-start.32 = (bf16[96,4096]{1,0:T(8,128)(2,1)S(1)}, bf16[96,4096]{1,0:T(8,128)(2,1)S(1)}, u32[]{:S(2)}, u32[]{:S(2)}) collective-permute-start(bf16[96,4096]{1,0:T(8,128)(2,1)S(1)} %copy-done.9), channel_id=1, source_target_pairs={{0,24},{8,16},{16,8},{24,0},{1,25},{9,17},{17,9},{25,1},{2,26},{10... | collective-permute-start | bytes 2359304 | tf_op jit(solution)/shard_map/ppermute | solution.py:563
  129.5 11.3 %collective-permute-start.29 = (bf16[128,512]{1,0:T(8,128)(2,1)S(1)}, bf16[128,512]{1,0:T(8,128)(2,1)S(1)}, u32[]{:S(2)}, u32[]{:S(2)}) collective-permute-start(bf16[128,512]{1,0:T(8,128)(2,1)S(1)} %get-tuple-element.74), channel_id=1, source_target_pairs={{0,6},{1,7},{2,0},{3,1},{4,2},{5,3},{6,4},{7,5},{8,14},{9,15},{10,... | collective-permute-start | bytes 393224 | tf_op jit(solution)/shard_map/ppermute | solution.py:558
  132.3 27.8 %collective-permute-start.33 = (bf16[96,4096]{1,0:T(8,128)(2,1)S(1)}, bf16[96,4096]{1,0:T(8,128)(2,1)}, u32[]{:S(2)}, u32[]{:S(2)}) collective-permute-start(bf16[96,4096]{1,0:T(8,128)(2,1)S(1)} %copy-done.9), channel_id=1, source_target_pairs={{0,16},{8,24},{16,0},{24,8},{1,17},{9,25},{17,1},{25,9},{2,18},{10... | collective-permute-start | bytes 2359304 | tf_op jit(solution)/shard_map/ppermute | solution.py:563
  133.3 26.8 %collective-permute-start.34 = (bf16[96,4096]{1,0:T(8,128)(2,1)S(1)}, bf16[96,4096]{1,0:T(8,128)(2,1)}, u32[]{:S(2)}, u32[]{:S(2)}) collective-permute-start(bf16[96,4096]{1,0:T(8,128)(2,1)S(1)} %copy-done.9), channel_id=1, source_target_pairs={{0,8},{8,0},{16,24},{24,16},{1,9},{9,1},{17,25},{25,17},{2,10},{10... | collective-permute-start | bytes 2359304 | tf_op jit(solution)/shard_map/ppermute | solution.py:563
  138.5 38.5 %collective-permute-start.35 = (bf16[96,4096]{1,0:T(8,128)(2,1)S(1)}, bf16[96,4096]{1,0:T(8,128)(2,1)}, u32[]{:S(2)}, u32[]{:S(2)}) collective-permute-start(bf16[96,4096]{1,0:T(8,128)(2,1)S(1)} %copy-done.8), channel_id=1, source_target_pairs={{0,24},{8,16},{16,8},{24,0},{1,25},{9,17},{17,9},{25,1},{2,26},{10... | collective-permute-start | bytes 2359304 | tf_op jit(solution)/shard_map/ppermute | solution.py:563
  140.8 52.1 %collective-permute-start.36 = (bf16[96,4096]{1,0:T(8,128)(2,1)S(1)}, bf16[96,4096]{1,0:T(8,128)(2,1)}, u32[]{:S(2)}, u32[]{:S(2)}) collective-permute-start(bf16[96,4096]{1,0:T(8,128)(2,1)S(1)} %copy-done.8), channel_id=1, source_target_pairs={{0,16},{8,24},{16,0},{24,8},{1,17},{9,25},{17,1},{25,9},{2,18},{10... | collective-permute-start | bytes 2359304 | tf_op jit(solution)/shard_map/ppermute | solution.py:563
  144.1 49.0 %collective-permute-start.37 = (bf16[96,4096]{1,0:T(8,128)(2,1)S(1)}, bf16[96,4096]{1,0:T(8,128)(2,1)}, u32[]{:S(2)}, u32[]{:S(2)}) collective-permute-start(bf16[96,4096]{1,0:T(8,128)(2,1)S(1)} %copy-done.8), channel_id=1, source_target_pairs={{0,8},{8,0},{16,24},{24,16},{1,9},{9,1},{17,25},{25,17},{2,10},{10... | collective-permute-start | bytes 2359304 | tf_op jit(solution)/shard_map/ppermute | solution.py:563
  (46 other events, 426.5 us)

commit v2 on v1

--- a/solution.py
+++ b/solution.py
@@ -277,12 +277,19 @@
     return grad_gate, grad_up, product
 
 
+def split_rows(rows_ref, halves):
+    part = halves[0].shape[0]
+    for i, half in enumerate(halves):
+        half[...] = rows_ref[i * part : (i + 1) * part]
+
+
 def early_kernel(n, *refs):
-    blocks, (weights, rows_ref, back_ref) = refs[:n], refs[n:]
+    blocks, (weights, *halves, back_ref, rows_ref) = refs[:n], refs[n:]
 
     @pl.when(pl.program_id(0) == 0)
     def _():
         unfold([(ref, PIECE if b > 2 and b % 2 else 0) for b, ref in enumerate(blocks)], rows_ref)
+        split_rows(rows_ref, halves)
 
     back_ref[...] = mm_t(rows_ref[...], weights[0])
 
@@ -294,10 +301,12 @@
     tile = 256
     return pl.pallas_call(
         lambda *refs: early_kernel(n, *refs),
-        out_shape=[jax.ShapeDtypeStruct((slots, width), BF16), jax.ShapeDtypeStruct((slots, hidden), F32)],
+        out_shape=[jax.ShapeDtypeStruct((slots // 2, width), BF16)] * 2
+        + [jax.ShapeDtypeStruct((slots, hidden), F32)],
         grid=(hidden // tile,),
+        scratch_shapes=[pltpu.VMEM((slots, width), BF16)],
         in_specs=[whole(b.shape) for b in blocks] + [pl.BlockSpec((1, tile, width), lambda i: (2, i, 0))],
-        out_specs=[whole((slots, width)), pl.BlockSpec((slots, tile), lambda i: (0, i))],
+        out_specs=[whole((slots // 2, width))] * 2 + [pl.BlockSpec((slots, tile), lambda i: (0, i))],
         compiler_params=params("arbitrary"),
         cost_estimate=pl.CostEstimate(flops=2 * 10**9, bytes_accessed=7 * 10**6, transcendentals=0),
         name="early",
@@ -305,13 +314,15 @@
 
 
 def expert_kernel(n, slots, *refs):
-    arrived, (back_ref, weights, routed_ref), blocks, acc_ref = refs[:n], refs[n : n + 3], refs[n + 3 : -1], refs[-1]
+    arrived, (back_ref, weights, *halves) = refs[:n], refs[n : n + 4]
+    blocks, (acc_ref, routed_ref) = refs[n + 4 : -2], refs[-2:]
     step = pl.program_id(0)
     width = acc_ref.shape[1]
 
     @pl.when(step == 0)
     def _():
         unfold([(ref, 0) for ref in arrived], routed_ref)
+        split_rows(routed_ref, halves)
 
     routed = routed_ref[...]
     gate_in = mm_t(routed, weights[0])
@@ -355,20 +366,21 @@
     half = width // FOLD
     outs = pl.pallas_call(
         lambda *refs: expert_kernel(n, slots, *refs),
-        out_shape=[jax.ShapeDtypeStruct((slots, width), BF16)] + [jax.ShapeDtypeStruct((PIECE, half), BF16)] * n,
+        out_shape=[jax.ShapeDtypeStruct((slots // 2, width), BF16)] * 2
+        + [jax.ShapeDtypeStruct((PIECE, half), BF16)] * n,
         grid=(hidden // tile,),
         in_specs=[whole(b.shape) for b in arrived]
         + [
             pl.BlockSpec((slots, tile), lambda i: (0, i)),
             pl.BlockSpec((2, tile, width), lambda i: (0, i, 0)),
         ],
-        out_specs=[whole((slots, width))] + [whole((PIECE, half))] * n,
-        scratch_shapes=[pltpu.VMEM((slots, width), F32)],
+        out_specs=[whole((slots // 2, width))] * 2 + [whole((PIECE, half))] * n,
+        scratch_shapes=[pltpu.VMEM((slots, width), F32), pltpu.VMEM((slots, width), BF16)],
         compiler_params=params("arbitrary"),
         cost_estimate=pl.CostEstimate(flops=8 * 10**9, bytes_accessed=2 * 10**7, transcendentals=0),
         name="expert",
     )(*arrived, back, weights)
-    return outs[0], list(outs[1:])
+    return outs[:2], list(outs[2:])
 
 
 def grads_kernel(count, share, dp_ref, *refs):
@@ -572,9 +584,19 @@
     return got
 
 
-def gather_docs(rows):
+def gather_docs(parts):
     n = lax.axis_size("dp")
-    return [rows] + [flip(rows, "dp", k) for k in range(n - 1, 0, -1)]
+    bits = [1 << b for b in range(n.bit_length() - 1)]
+    got = []
+    for part, order in zip(parts, (bits, bits[::-1])):
+        pieces = [part]
+        for bit in order:
+            moved = []
+            for piece in pieces:
+                moved.append(flip(piece, "dp", bit))
+            pieces += moved
+        got += pieces
+    return got
 
 
 def per_device(
@@ -608,7 +630,7 @@
     grad_blocks = [grad_blocks[0], flip(grad_blocks[1], "ctx", 1)]
     for pair in pairs:
         grad_blocks += [pair, flip(pair, "ctx", 1)]
-    weighted, back_rows = early(grad_blocks, weights)
+    *weighted, back_rows = early(grad_blocks, weights)
     all_weighted = gather_docs(weighted)
 
     fwd, row_blocks = forward(me, span_order, kv_blocks, query[0], pick, gain)

time: 205 us -> 192 us (0.937)
  waiting for transfers between devices: 87.5 us -> 73.5 us
    ppermute x15 -> x21, waiting for transfers between devices: 48.6 us -> 38.2 us  [flip(): return lax.ppermute(x, axis, [(i, i ^ bit) for i in range(n)])]
    ppermute x9, waiting for transfers between devices: 22 us -> 18.4 us  [shift(): return lax.ppermute(x, axis, [(i, (i + k) % n) for i in range(n)])]
    ppermute x15 -> x21, starting transfers between devices: 12.2 us -> 15.1 us  [flip(): return lax.ppermute(x, axis, [(i, i ^ bit) for i in range(n)])]
    ppermute x9, starting transfers between devices: 16.2 us -> 13.9 us  [shift(): return lax.ppermute(x, axis, [(i, (i + k) % n) for i in range(n)])]
  transfers between devices with their start and end apart: 38 -> 44, of which waited for: 13 -> 16; matrix products, arithmetic and copies ran while one was open for 1% -> 1% of each run, Pallas kernels for 11% -> 12%
where the time goes in v2:
time: 192 us
  waiting for transfers between devices  73.5 us (38%)
  Pallas kernels  61.8 us (32%)
  starting transfers between devices  49.4 us (26%)
  local copies, waits for them, and re-layouts  3.42 us (2%)
  other arithmetic  2.39 us (1%)
    ppermute x21, waiting for transfers between devices, flip(): return lax.ppermute(x, axis, [(i, i ^ bit) for i in range(n)])  38.2 us
    ppermute x14, starting transfers between devices, exchange(): lax.ppermute(blocks[b], 'ctx', [(i, peer_of(i, b, n, sign)) for i in rang...  20.3 us
    ppermute x9, waiting for transfers between devices, shift(): return lax.ppermute(x, axis, [(i, (i + k) % n) for i in range(n)])  18.4 us
    ppermute x14, waiting for transfers between devices, exchange(): lax.ppermute(blocks[b], 'ctx', [(i, peer_of(i, b, n, sign)) for i in rang...  16.9 us
    pallas_call x1, Pallas kernels, backward(): pl.pallas_call(lambda *refs: backward_kernel(n, rows, width, *refs), out_...  15.1 us
    ppermute x21, starting transfers between devices, flip(): return lax.ppermute(x, axis, [(i, i ^ bit) for i in range(n)])  15.1 us
    pallas_call x1, Pallas kernels, forward(): pl.pallas_call(lambda *refs: forward_kernel(n, rows, width, *refs), out_s...  14.1 us
    ppermute x9, starting transfers between devices, shift(): return lax.ppermute(x, axis, [(i, (i + k) % n) for i in range(n)])  13.9 us
  transfers between devices with their start and end apart: 44, of which 16 were waited for; matrix products, arithmetic and copies ran while one was open for 1% of the time, Pallas kernels for 12%

profile of v2, /device:TPU:0, one launch (start us, length us, event | category | flops | bytes accessed | tf_op | source)
XLA Modules:
  0.0 191.6 jit_solution(9357452169726653478)
XLA Ops:
  2.1 2.6 %collective-permute-start.1 = (bf16[128,512]{1,0:T(8,128)(2,1)S(1)}, bf16[128,512]{1,0:T(8,128)(2,1)S(1)}, u32[]{:S(2)}, u32[]{:S(2)}) collective-permute-start(bf16[128,512]{1,0:T(8,128)(2,1)S(1)} %pad_maximum_fusion.refs_2_), channel_id=1, source_target_pairs={{0,2},{1,3},{2,4},{3,5},{4,6},{5,7},{6,0},{7,1},{8,10},{9,11},{10,... | collective-permute-start | bytes 393224 | tf_op jit(solution)/shard_map/ppermute | solution.py:570
  4.7 2.8 %route.1 = (bf16[2,192,128]{2,1,0:T(8,128)(2,1)}, bf16[24,2048]{1,0:T(8,128)(2,1)}, bf16[24,2048]{1,0:T(8,128)(2,1)}, bf16[48,2048]{1,0:T(8,128)(2,1)}, bf16[48,...) custom-call(s32[1]{0:T(128)} %bitcast.refs_0_, s32[8]{0:T(128)} %refs_1_.2, s32[8,128]{1,0:T(8,128)} %bitcast.51, ...), custom_call_target="tpu_custom_call" | custom-call | flops 4000000000 | bytes 2000000 | tf_op jit(solution)/shard_map/route/pallas_call | solution.py:106
  10.1 2.9 %collective-permute-start.5 = (bf16[128,512]{1,0:T(8,128)(2,1)S(1)}, bf16[128,512]{1,0:T(8,128)(2,1)S(1)}, u32[]{:S(2)}, u32[]{:S(2)}) collective-permute-start(bf16[128,512]{1,0:T(8,128)(2,1)S(1)} %pad_maximum_fusion.refs_2_), channel_id=1, source_target_pairs={{0,6},{1,7},{2,0},{3,1},{4,2},{5,3},{6,4},{7,5},{8,14},{9,15},{10,... | collective-permute-start | bytes 393224 | tf_op jit(solution)/shard_map/ppermute | solution.py:570
  14.5 8.6 %collective-permute-done.3.refs_6_ = bf16[128,512]{1,0:T(8,128)(2,1)S(1)} collective-permute-done((bf16[128,512]{1,0:T(8,128)(2,1)S(1)}, bf16[128,512]{1,0:T(8,128)(2,1)S(1)}, u32[]{:S(2)}, u32[]{:S(2)}) %collective-permute-start.3) | collective-permute-done | bytes 131104 | tf_op jit(solution)/shard_map/ppermute | solution.py:570
  23.7 9.8 %collective-permute-done.17.refs_4_ = bf16[48,2048]{1,0:T(8,128)(2,1)S(1)} collective-permute-done((bf16[48,2048]{1,0:T(8,128)(2,1)}, bf16[48,2048]{1,0:T(8,128)(2,1)S(1)}, u32[]{:S(2)}, u32[]{:S(2)}) %collective-permute-start.17) | collective-permute-done | bytes 196640 | tf_op jit(solution)/shard_map/ppermute | solution.py:570
  35.2 14.1 %forward.1 = (bf16[2,1024,256]{2,1,0:T(8,128)(2,1)}, bf16[2,1024,256]{2,1,0:T(8,128)(2,1)}, bf16[2,128,1024]{2,1,0:T(8,128)(2,1)}, bf16[2,144,1024]{2,1,0:T(8,12...) custom-call(s32[1]{0:T(128)} %bitcast.refs_0_, ...), custom_call_target="tpu_custom_call" | custom-call | flops 10000000000 | bytes 20000000 | tf_op jit(solution)/shard_map/forward/pallas_call | solution.py:255
  49.5 4.6 %collective-permute-start.8 = (bf16[24,2048]{1,0:T(8,128)(2,1)}, bf16[24,2048]{1,0:T(8,128)(2,1)S(1)}, u32[]{:S(2)}, u32[]{:S(2)}) collective-permute-start(bf16[24,2048]{1,0:T(8,128)(2,1)} %get-tuple-element.43), channel_id=1, source_target_pairs={{0,2},{1,3},{2,4},{3,5},{4,6},{5,7},{6,0},{7,1},{8,10},{9,11},{10,... | collective-permute-start | bytes 294920 | tf_op jit(solution)/shard_map/ppermute | solution.py:583
  55.2 3.6 %collective-permute-done.8.refs_2_ = bf16[24,2048]{1,0:T(8,128)(2,1)S(1)} collective-permute-done((bf16[24,2048]{1,0:T(8,128)(2,1)}, bf16[24,2048]{1,0:T(8,128)(2,1)S(1)}, u32[]{:S(2)}, u32[]{:S(2)}) %collective-permute-start.8) | collective-permute-done | bytes 98336 | tf_op jit(solution)/shard_map/ppermute | solution.py:583
  63.9 6.2 %early.1 = (bf16[48,4096]{1,0:T(8,128)(2,1)}, bf16[48,4096]{1,0:T(8,128)(2,1)}, f32[96,768]{1,0:T(8,128)}) custom-call(bf16[24,2048]{1,0:T(8,128)(2,1)} %get-tuple-element.49.refs_0_, bf16[24,2048]{1,0:T(8,128)(2,1)} %copy-done.7, bf16[48,2048]{1,0:T(8,128)(2,1)} %copy-done, bf16[48,2048]{1,0:T(8,128)(2,1)} %copy-done.3, bf16[48,2048]{1,0:T(8,128)(2,1)} %copy-done.1, ...), custom_call_target="tpu_custom_call" | custom-call | flops 2000000000 | bytes 7000000 | tf_op jit(solution)/shard_map/early/pallas_call | solution.py:302
  72.0 11.7 %expert.1 = (bf16[48,4096]{1,0:T(8,128)(2,1)}, bf16[48,4096]{1,0:T(8,128)(2,1)}, bf16[24,2048]{1,0:T(8,128)(2,1)}, bf16[24,2048]{1,0:T(8,128)(2,1)}, bf16[24,204...) custom-call(bf16[24,2048]{1,0:T(8,128)(2,1)} %get-tuple-element.41.r, ...), custom_call_target="tpu_custom_call" | custom-call | flops 8000000000 | bytes 20000000 | tf_op jit(solution)/shard_map/expert/pallas_call | solution.py:367
  83.9 4.6 %collective-permute-start.22 = (bf16[24,2048]{1,0:T(8,128)(2,1)}, bf16[24,2048]{1,0:T(8,128)(2,1)S(1)}, u32[]{:S(2)}, u32[]{:S(2)}) collective-permute-start(bf16[24,2048]{1,0:T(8,128)(2,1)} %get-tuple-element.57), channel_id=1, source_target_pairs={{0,6},{1,7},{2,0},{3,1},{4,2},{5,3},{6,4},{7,5},{8,14},{9,15},{10,... | collective-permute-start | bytes 294920 | tf_op jit(solution)/shard_map/ppermute | solution.py:583
  88.5 2.4 %collective-permute-start.25 = (bf16[24,2048]{1,0:T(8,128)(2,1)}, bf16[24,2048]{1,0:T(8,128)(2,1)S(1)}, u32[]{:S(2)}, u32[]{:S(2)}) collective-permute-start(bf16[24,2048]{1,0:T(8,128)(2,1)} %get-tuple-element.60), channel_id=1, source_target_pairs={{0,5},{1,4},{2,7},{3,6},{4,1},{5,0},{6,3},{7,2},{8,13},{9,12},{10,... | collective-permute-start | bytes 294920 | tf_op jit(solution)/shard_map/ppermute | solution.py:583
  90.9 2.0 %collective-permute-start.26 = (bf16[24,2048]{1,0:T(8,128)(2,1)}, bf16[24,2048]{1,0:T(8,128)(2,1)S(1)}, u32[]{:S(2)}, u32[]{:S(2)}) collective-permute-start(bf16[24,2048]{1,0:T(8,128)(2,1)} %get-tuple-element.61), channel_id=1, source_target_pairs={{0,2},{1,3},{2,4},{3,5},{4,6},{5,7},{6,0},{7,1},{8,10},{9,11},{10,... | collective-permute-start | bytes 294920 | tf_op jit(solution)/shard_map/ppermute | solution.py:583
  94.3 10.6 %collective-permute-done.24.refs_4_ = bf16[24,2048]{1,0:T(8,128)(2,1)S(1)} collective-permute-done((bf16[24,2048]{1,0:T(8,128)(2,1)}, bf16[24,2048]{1,0:T(8,128)(2,1)S(1)}, u32[]{:S(2)}, u32[]{:S(2)}) %collective-permute-start.24) | collective-permute-done | bytes 98336 | tf_op jit(solution)/shard_map/ppermute | solution.py:583
  105.9 15.1 %backward.1 = (bf16[128,4096]{1,0:T(8,128)(2,1)}, f32[4,128,512]{2,1,0:T(8,128)}, bf16[4,128,512]{2,1,0:T(8,128)(2,1)}) custom-call(bf16[24,2048]{1,0:T(8,128)(2,1)} %get-tuple-element.55.refs_0_, bf16[24,2048]{1,0:T(8,128)(2,1)} %copy-done.30, bf16[24,2048]{1,0:T(8,128)(2,1)} %copy-done.32, bf16[24,2048]{1,0:T(8,128)(2,1)} %copy-done.33, ...), custom_call_target="tpu_custom_call" | custom-call | flops 20000000000 | bytes 20000000 | tf_op jit(solution)/shard_map/backward/pallas_call | solution.py:538
  125.9 7.9 %collective-permute-done.32.refs_2_ = bf16[48,4096]{1,0:T(8,128)(2,1)S(1)} collective-permute-done((bf16[48,4096]{1,0:T(8,128)(2,1)S(1)}, bf16[48,4096]{1,0:T(8,128)(2,1)S(1)}, u32[]{:S(2)}, u32[]{:S(2)}) %collective-permute-start.32) | collective-permute-done | bytes 393248 | tf_op jit(solution)/shard_map/ppermute | solution.py:575
  138.9 4.9 %collective-permute-done.35.refs_6_ = bf16[48,4096]{1,0:T(8,128)(2,1)S(1)} collective-permute-done((bf16[48,4096]{1,0:T(8,128)(2,1)S(1)}, bf16[48,4096]{1,0:T(8,128)(2,1)S(1)}, u32[]{:S(2)}, u32[]{:S(2)}) %collective-permute-start.35) | collective-permute-done | bytes 393248 | tf_op jit(solution)/shard_map/ppermute | solution.py:575
  145.5 1.9 collective-permute-start.30
  147.4 2.4 %collective-permute-done.38.refs_10_ = bf16[48,4096]{1,0:T(8,128)(2,1)S(1)} collective-permute-done((bf16[48,4096]{1,0:T(8,128)(2,1)S(1)}, bf16[48,4096]{1,0:T(8,128)(2,1)S(1)}, u32[]{:S(2)}, u32[]{:S(2)}) %collective-permute-start.38) | collective-permute-done | bytes 393248 | tf_op jit(solution)/shard_map/ppermute | solution.py:575
  152.8 6.7 %collective-permute-done.41.refs_14_ = bf16[48,4096]{1,0:T(8,128)(2,1)} collective-permute-done((bf16[48,4096]{1,0:T(8,128)(2,1)S(1)}, bf16[48,4096]{1,0:T(8,128)(2,1)}, u32[]{:S(2)}, u32[]{:S(2)}) %collective-permute-start.41) | collective-permute-done | bytes 393248 | tf_op jit(solution)/shard_map/ppermute | solution.py:575
  164.4 7.2 %collective-permute-done.34.refs_4_ = bf16[48,4096]{1,0:T(8,128)(2,1)S(1)} collective-permute-done((bf16[48,4096]{1,0:T(8,128)(2,1)S(1)}, bf16[48,4096]{1,0:T(8,128)(2,1)S(1)}, u32[]{:S(2)}, u32[]{:S(2)}) %collective-permute-start.34) | collective-permute-done | bytes 393248 | tf_op jit(solution)/shard_map/ppermute | solution.py:575
  171.6 1.8 collective-permute-done.37.refs_8_
  173.4 4.7 %collective-permute-done.40.refs_12_ = bf16[48,4096]{1,0:T(8,128)(2,1)} collective-permute-done((bf16[48,4096]{1,0:T(8,128)(2,1)}, bf16[48,4096]{1,0:T(8,128)(2,1)}, u32[]{:S(2)}, u32[]{:S(2)}) %collective-permute-start.40) | collective-permute-done | bytes 393248 | tf_op jit(solution)/shard_map/ppermute | solution.py:575
  179.5 11.9 %grads.1 = bf16[3,192,4096]{2,1,0:T(8,128)(2,1)} custom-call(s32[1]{0:T(128)} %bitcast.19.refs_0_, bf16[48,4096]{1,0:T(8,128)(2,1)} %get-tuple-element.72.refs_1_, bf16[48,4096]{1,0:T(8,128)(2,1)} %copy-done.12, bf16[48,4096]{1,0:T(8,128)(2,1)} %copy-done.13, bf16[48,4096]{1,0:T(8,128)(2,1)} %copy-done.18, bf16[48,4096]{1,0:T(8,128)(2,1)} %get-tuple-element.73.refs_5_, ...), custom_call_target="tpu_custom_call" | custom-call | flops 10000000000 | bytes 15000000 | tf_op jit(solution)/shard_map/grads/pallas_call | solution.py:430
  (155 shorter events, 39.4 us)
Async XLA Ops:
  7.5 16.1 %collective-permute-start.15 = (bf16[48,2048]{1,0:T(8,128)(2,1)}, bf16[48,2048]{1,0:T(8,128)(2,1)S(1)}, u32[]{:S(2)}, u32[]{:S(2)}) collective-permute-start(bf16[48,2048]{1,0:T(8,128)(2,1)} %get-tuple-element.51), channel_id=1, source_target_pairs={{0,2},{1,3},{2,4},{3,5},{4,6},{5,7},{6,0},{7,1},{8,10},{9,11},{10,... | collective-permute-start | bytes 589832 | tf_op jit(solution)/shard_map/ppermute | solution.py:570
  9.1 14.0 %collective-permute-start.3 = (bf16[128,512]{1,0:T(8,128)(2,1)S(1)}, bf16[128,512]{1,0:T(8,128)(2,1)S(1)}, u32[]{:S(2)}, u32[]{:S(2)}) collective-permute-start(bf16[128,512]{1,0:T(8,128)(2,1)S(1)} %pad_maximum_fusion.refs_2_), channel_id=1, source_target_pairs={{0,4},{1,5},{2,6},{3,7},{4,0},{5,1},{6,2},{7,3},{8,12},{9,13},{10,... | collective-permute-start | bytes 393224 | tf_op jit(solution)/shard_map/ppermute | solution.py:570
  10.1 13.0 %collective-permute-start.5 = (bf16[128,512]{1,0:T(8,128)(2,1)S(1)}, bf16[128,512]{1,0:T(8,128)(2,1)S(1)}, u32[]{:S(2)}, u32[]{:S(2)}) collective-permute-start(bf16[128,512]{1,0:T(8,128)(2,1)S(1)} %pad_maximum_fusion.refs_2_), channel_id=1, source_target_pairs={{0,6},{1,7},{2,0},{3,1},{4,2},{5,3},{6,4},{7,5},{8,14},{9,15},{10,... | collective-permute-start | bytes 393224 | tf_op jit(solution)/shard_map/ppermute | solution.py:570
  13.0 20.5 %collective-permute-start.17 = (bf16[48,2048]{1,0:T(8,128)(2,1)}, bf16[48,2048]{1,0:T(8,128)(2,1)S(1)}, u32[]{:S(2)}, u32[]{:S(2)}) collective-permute-start(bf16[48,2048]{1,0:T(8,128)(2,1)} %get-tuple-element.52), channel_id=1, source_target_pairs={{0,4},{1,5},{2,6},{3,7},{4,0},{5,1},{6,2},{7,3},{8,12},{9,13},{10,... | collective-permute-start | bytes 589832 | tf_op jit(solution)/shard_map/ppermute | solution.py:570
  13.4 20.2 %collective-permute-start.19 = (bf16[48,2048]{1,0:T(8,128)(2,1)}, bf16[48,2048]{1,0:T(8,128)(2,1)S(1)}, u32[]{:S(2)}, u32[]{:S(2)}) collective-permute-start(bf16[48,2048]{1,0:T(8,128)(2,1)} %get-tuple-element.53), channel_id=1, source_target_pairs={{0,6},{1,7},{2,0},{3,1},{4,2},{5,3},{6,4},{7,5},{8,14},{9,15},{10,... | collective-permute-start | bytes 589832 | tf_op jit(solution)/shard_map/ppermute | solution.py:570
  33.5 16.0 %collective-permute-start.14 = (bf16[24,2048]{1,0:T(8,128)(2,1)}, bf16[24,2048]{1,0:T(8,128)(2,1)S(1)}, u32[]{:S(2)}, u32[]{:S(2)}) collective-permute-start(bf16[24,2048]{1,0:T(8,128)(2,1)} %get-tuple-element.50), channel_id=1, source_target_pairs={{0,1},{1,0},{2,3},{3,2},{4,5},{5,4},{6,7},{7,6},{8,9},{9,8},{10,11... | collective-permute-start | bytes 294920 | tf_op jit(solution)/shard_map/ppermute | solution.py:575
  33.5 25.8 %collective-permute-start.16 = (bf16[48,2048]{1,0:T(8,128)(2,1)S(1)}, bf16[48,2048]{1,0:T(8,128)(2,1)S(1)}, u32[]{:S(2)}, u32[]{:S(2)}) collective-permute-start(bf16[48,2048]{1,0:T(8,128)(2,1)S(1)} %collective-permute-done.15.refs_2_), channel_id=1, source_target_pairs={{0,1},{1,0},{2,3},{3,2},{4,5},{5,4},{6,7},{7,6},{8,9},{9,8},{10,11... | collective-permute-start | bytes 589832 | tf_op jit(solution)/shard_map/ppermute | solution.py:575
  34.0 26.9 %collective-permute-start.18 = (bf16[48,2048]{1,0:T(8,128)(2,1)S(1)}, bf16[48,2048]{1,0:T(8,128)(2,1)S(1)}, u32[]{:S(2)}, u32[]{:S(2)}) collective-permute-start(bf16[48,2048]{1,0:T(8,128)(2,1)S(1)} %collective-permute-done.17.refs_4_), channel_id=1, source_target_pairs={{0,1},{1,0},{2,3},{3,2},{4,5},{5,4},{6,7},{7,6},{8,9},{9,8},{10,11... | collective-permute-start | bytes 589832 | tf_op jit(solution)/shard_map/ppermute | solution.py:575
  34.1 28.3 %collective-permute-start.20 = (bf16[48,2048]{1,0:T(8,128)(2,1)S(1)}, bf16[48,2048]{1,0:T(8,128)(2,1)S(1)}, u32[]{:S(2)}, u32[]{:S(2)}) collective-permute-start(bf16[48,2048]{1,0:T(8,128)(2,1)S(1)} %collective-permute-done.19.refs_6_), channel_id=1, source_target_pairs={{0,1},{1,0},{2,3},{3,2},{4,5},{5,4},{6,7},{7,6},{8,9},{9,8},{10,11... | collective-permute-start | bytes 589832 | tf_op jit(solution)/shard_map/ppermute | solution.py:575
  54.1 15.9 %collective-permute-start.9 = (bf16[24,2048]{1,0:T(8,128)(2,1)}, bf16[24,2048]{1,0:T(8,128)(2,1)S(1)}, u32[]{:S(2)}, u32[]{:S(2)}) collective-permute-start(bf16[24,2048]{1,0:T(8,128)(2,1)} %get-tuple-element.44), channel_id=1, source_target_pairs={{0,3},{1,2},{2,5},{3,4},{4,7},{5,6},{6,1},{7,0},{8,11},{9,10},{10,... | collective-permute-start | bytes 294920 | tf_op jit(solution)/shard_map/ppermute | solution.py:583
  88.5 16.4 %collective-permute-start.24 = (bf16[24,2048]{1,0:T(8,128)(2,1)}, bf16[24,2048]{1,0:T(8,128)(2,1)S(1)}, u32[]{:S(2)}, u32[]{:S(2)}) collective-permute-start(bf16[24,2048]{1,0:T(8,128)(2,1)} %get-tuple-element.59), channel_id=1, source_target_pairs={{0,4},{1,5},{2,6},{3,7},{4,0},{5,1},{6,2},{7,3},{8,12},{9,13},{10,... | collective-permute-start | bytes 294920 | tf_op jit(solution)/shard_map/ppermute | solution.py:583
  88.5 16.7 %collective-permute-start.25 = (bf16[24,2048]{1,0:T(8,128)(2,1)}, bf16[24,2048]{1,0:T(8,128)(2,1)S(1)}, u32[]{:S(2)}, u32[]{:S(2)}) collective-permute-start(bf16[24,2048]{1,0:T(8,128)(2,1)} %get-tuple-element.60), channel_id=1, source_target_pairs={{0,5},{1,4},{2,7},{3,6},{4,1},{5,0},{6,3},{7,2},{8,13},{9,12},{10,... | collective-permute-start | bytes 294920 | tf_op jit(solution)/shard_map/ppermute | solution.py:583
  90.9 14.3 %collective-permute-start.26 = (bf16[24,2048]{1,0:T(8,128)(2,1)}, bf16[24,2048]{1,0:T(8,128)(2,1)S(1)}, u32[]{:S(2)}, u32[]{:S(2)}) collective-permute-start(bf16[24,2048]{1,0:T(8,128)(2,1)} %get-tuple-element.61), channel_id=1, source_target_pairs={{0,2},{1,3},{2,4},{3,5},{4,6},{5,7},{6,0},{7,1},{8,10},{9,11},{10,... | collective-permute-start | bytes 294920 | tf_op jit(solution)/shard_map/ppermute | solution.py:583
  121.0 15.8 %collective-permute-start.28 = (bf16[4,128,512]{2,1,0:T(8,128)(2,1)}, bf16[4,128,512]{2,1,0:T(8,128)(2,1)S(1)}, u32[]{:S(2)}, u32[]{:S(2)}) collective-permute-start(bf16[4,128,512]{2,1,0:T(8,128)(2,1)} %get-tuple-element.71), channel_id=1, source_target_pairs={{0,1},{1,0},{2,3},{3,2},{4,5},{5,4},{6,7},{7,6},{8,9},{9,8},{10,11... | collective-permute-start | bytes 1572872 | tf_op jit(solution)/shard_map/ppermute | solution.py:575
  124.9 18.9 %collective-permute-start.35 = (bf16[48,4096]{1,0:T(8,128)(2,1)S(1)}, bf16[48,4096]{1,0:T(8,128)(2,1)S(1)}, u32[]{:S(2)}, u32[]{:S(2)}) collective-permute-start(bf16[48,4096]{1,0:T(8,128)(2,1)S(1)} %copy-done.11), channel_id=1, source_target_pairs={{0,16},{8,24},{16,0},{24,8},{1,17},{9,25},{17,1},{25,9},{2,18},{10... | collective-permute-start | bytes 1179656 | tf_op jit(solution)/shard_map/ppermute | solution.py:575
  125.4 20.1 %collective-permute-start.36 = (bf16[48,4096]{1,0:T(8,128)(2,1)S(1)}, bf16[48,4096]{1,0:T(8,128)(2,1)S(1)}, u32[]{:S(2)}, u32[]{:S(2)}) collective-permute-start(bf16[48,4096]{1,0:T(8,128)(2,1)S(1)} %copy-done.11), channel_id=1, source_target_pairs={{0,8},{8,0},{16,24},{24,16},{1,9},{9,1},{17,25},{25,17},{2,10},{10... | collective-permute-start | bytes 1179656 | tf_op jit(solution)/shard_map/ppermute | solution.py:575
  133.8 16.0 %collective-permute-start.38 = (bf16[48,4096]{1,0:T(8,128)(2,1)S(1)}, bf16[48,4096]{1,0:T(8,128)(2,1)S(1)}, u32[]{:S(2)}, u32[]{:S(2)}) collective-permute-start(bf16[48,4096]{1,0:T(8,128)(2,1)S(1)} %copy-done.8), channel_id=1, source_target_pairs={{0,8},{8,0},{16,24},{24,16},{1,9},{9,1},{17,25},{25,17},{2,10},{10... | collective-permute-start | bytes 1179656 | tf_op jit(solution)/shard_map/ppermute | solution.py:575
  135.4 16.9 %collective-permute-start.39 = (bf16[48,4096]{1,0:T(8,128)(2,1)S(1)}, bf16[48,4096]{1,0:T(8,128)(2,1)}, u32[]{:S(2)}, u32[]{:S(2)}) collective-permute-start(bf16[48,4096]{1,0:T(8,128)(2,1)S(1)} %copy-done.8), channel_id=1, source_target_pairs={{0,16},{8,24},{16,0},{24,8},{1,17},{9,25},{17,1},{25,9},{2,18},{10... | collective-permute-start | bytes 1179656 | tf_op jit(solution)/shard_map/ppermute | solution.py:575
  136.9 22.7 %collective-permute-start.41 = (bf16[48,4096]{1,0:T(8,128)(2,1)S(1)}, bf16[48,4096]{1,0:T(8,128)(2,1)}, u32[]{:S(2)}, u32[]{:S(2)}) collective-permute-start(bf16[48,4096]{1,0:T(8,128)(2,1)S(1)} %copy-done.9), channel_id=1, source_target_pairs={{0,16},{8,24},{16,0},{24,8},{1,17},{9,25},{17,1},{25,9},{2,18},{10... | collective-permute-start | bytes 1179656 | tf_op jit(solution)/shard_map/ppermute | solution.py:575
  143.8 17.3 %collective-permute-start.31 = (bf16[128,512]{1,0:T(8,128)(2,1)S(1)}, bf16[128,512]{1,0:T(8,128)(2,1)S(1)}, u32[]{:S(2)}, u32[]{:S(2)}) collective-permute-start(bf16[128,512]{1,0:T(8,128)(2,1)S(1)} %get-tuple-element.79), channel_id=1, source_target_pairs={{0,2},{1,3},{2,4},{3,5},{4,6},{5,7},{6,0},{7,1},{8,10},{9,11},{10,... | collective-permute-start | bytes 393224 | tf_op jit(solution)/shard_map/ppermute | solution.py:570
  145.5 16.1 %collective-permute-start.30 = (bf16[128,512]{1,0:T(8,128)(2,1)S(1)}, bf16[128,512]{1,0:T(8,128)(2,1)S(1)}, u32[]{:S(2)}, u32[]{:S(2)}) collective-permute-start(bf16[128,512]{1,0:T(8,128)(2,1)S(1)} %get-tuple-element.80), channel_id=1, source_target_pairs={{0,4},{1,5},{2,6},{3,7},{4,0},{5,1},{6,2},{7,3},{8,12},{9,13},{10,... | collective-permute-start | bytes 393224 | tf_op jit(solution)/shard_map/ppermute | solution.py:570
  161.1 12.3 %collective-permute-start.37 = (bf16[48,4096]{1,0:T(8,128)(2,1)}, bf16[48,4096]{1,0:T(8,128)(2,1)}, u32[]{:S(2)}, u32[]{:S(2)}) collective-permute-start(bf16[48,4096]{1,0:T(8,128)(2,1)} %copy-done.14), channel_id=1, source_target_pairs={{0,8},{8,0},{16,24},{24,16},{1,9},{9,1},{17,25},{25,17},{2,10},{10... | collective-permute-start | bytes 1179656 | tf_op jit(solution)/shard_map/ppermute | solution.py:575
  161.6 16.5 %collective-permute-start.40 = (bf16[48,4096]{1,0:T(8,128)(2,1)}, bf16[48,4096]{1,0:T(8,128)(2,1)}, u32[]{:S(2)}, u32[]{:S(2)}) collective-permute-start(bf16[48,4096]{1,0:T(8,128)(2,1)} %copy-done.16), channel_id=1, source_target_pairs={{0,16},{8,24},{16,0},{24,8},{1,17},{9,25},{17,1},{25,9},{2,18},{10... | collective-permute-start | bytes 1179656 | tf_op jit(solution)/shard_map/ppermute | solution.py:575
  162.1 17.4 %collective-permute-start.43 = (bf16[48,4096]{1,0:T(8,128)(2,1)}, bf16[48,4096]{1,0:T(8,128)(2,1)}, u32[]{:S(2)}, u32[]{:S(2)}) collective-permute-start(bf16[48,4096]{1,0:T(8,128)(2,1)} %collective-permute-done.41.refs_14_), channel_id=1, source_target_pairs={{0,8},{8,0},{16,24},{24,16},{1,9},{9,1},{17,25},{25,17},{2,10},{10... | collective-permute-start | bytes 1179656 | tf_op jit(solution)/shard_map/ppermute | solution.py:575
  (60 other events, 679.1 us)

commit v3 on v2

--- a/solution.py
+++ b/solution.py
@@ -16,6 +16,7 @@
 FOLD = 2
 PIECE = FOLD * CAP
 STEP_HEADS = 8
+VMEM_BYTES = 67043328
 F32 = jnp.float32
 BF16 = jnp.bfloat16
 
@@ -38,8 +39,8 @@
 
 def params(*semantics):
     if semantics:
-        return pltpu.CompilerParams(dimension_semantics=semantics, vmem_limit_bytes=60 << 20)
-    return pltpu.CompilerParams(vmem_limit_bytes=60 << 20)
+        return pltpu.CompilerParams(dimension_semantics=semantics, vmem_limit_bytes=VMEM_BYTES)
+    return pltpu.CompilerParams(vmem_limit_bytes=VMEM_BYTES)
 
 
 def whole(shape):

time: 192 us -> 192 us (level)
  no operation moved by 1% of the time
where the time goes in v3:
time: 192 us
  waiting for transfers between devices  74.1 us (39%)
  Pallas kernels  61.6 us (32%)
  starting transfers between devices  49.3 us (26%)
  other arithmetic  3.03 us (2%)
  local copies, waits for them, and re-layouts  2.82 us (1%)
    ppermute x21, waiting for transfers between devices, flip(): return lax.ppermute(x, axis, [(i, i ^ bit) for i in range(n)])  38.6 us
    ppermute x14, starting transfers between devices, exchange(): lax.ppermute(blocks[b], 'ctx', [(i, peer_of(i, b, n, sign)) for i in rang...  20.2 us
    ppermute x9, waiting for transfers between devices, shift(): return lax.ppermute(x, axis, [(i, (i + k) % n) for i in range(n)])  18.1 us
    ppermute x14, waiting for transfers between devices, exchange(): lax.ppermute(blocks[b], 'ctx', [(i, peer_of(i, b, n, sign)) for i in rang...  17.4 us
    pallas_call x1, Pallas kernels, backward(): pl.pallas_call(lambda *refs: backward_kernel(n, rows, width, *refs), out_...  15.1 us
    ppermute x21, starting transfers between devices, flip(): return lax.ppermute(x, axis, [(i, i ^ bit) for i in range(n)])  15.1 us
    pallas_call x1, Pallas kernels, forward(): pl.pallas_call(lambda *refs: forward_kernel(n, rows, width, *refs), out_s...  14.1 us
    ppermute x9, starting transfers between devices, shift(): return lax.ppermute(x, axis, [(i, (i + k) % n) for i in range(n)])  14.1 us
  transfers between devices with their start and end apart: 44, of which 16 were waited for; matrix products, arithmetic and copies ran while one was open for 1% of the time, Pallas kernels for 12%

profile of v3, /device:TPU:0, one launch (start us, length us, event | category | flops | bytes accessed | tf_op | source)
XLA Modules:
  0.0 191.8 jit_solution(7354373025521009282)
XLA Ops:
  2.6 2.6 %collective-permute-start.1 = (bf16[128,512]{1,0:T(8,128)(2,1)}, bf16[128,512]{1,0:T(8,128)(2,1)}, u32[]{:S(2)}, u32[]{:S(2)}) collective-permute-start(bf16[128,512]{1,0:T(8,128)(2,1)} %pad_maximum_fusion.refs_2_), channel_id=1, source_target_pairs={{0,2},{1,3},{2,4},{3,5},{4,6},{5,7},{6,0},{7,1},{8,10},{9,11},{10,... | collective-permute-start | bytes 393224 | tf_op jit(solution)/shard_map/ppermute | solution.py:571
  5.2 2.8 %route.1 = (bf16[2,192,128]{2,1,0:T(8,128)(2,1)}, bf16[24,2048]{1,0:T(8,128)(2,1)}, bf16[24,2048]{1,0:T(8,128)(2,1)}, bf16[48,2048]{1,0:T(8,128)(2,1)}, bf16[48,...) custom-call(s32[1]{0:T(128)} %bitcast.refs_0_, s32[8]{0:T(128)} %refs_1_.2, s32[8,128]{1,0:T(8,128)} %bitcast.51, ...), custom_call_target="tpu_custom_call" | custom-call | flops 4000000000 | bytes 2000000 | tf_op jit(solution)/shard_map/route/pallas_call | solution.py:107
  10.6 2.9 %collective-permute-start.5 = (bf16[128,512]{1,0:T(8,128)(2,1)}, bf16[128,512]{1,0:T(8,128)(2,1)S(1)}, u32[]{:S(2)}, u32[]{:S(2)}) collective-permute-start(bf16[128,512]{1,0:T(8,128)(2,1)} %pad_maximum_fusion.refs_2_), channel_id=1, source_target_pairs={{0,6},{1,7},{2,0},{3,1},{4,2},{5,3},{6,4},{7,5},{8,14},{9,15},{10,... | collective-permute-start | bytes 393224 | tf_op jit(solution)/shard_map/ppermute | solution.py:571
  15.0 8.6 %collective-permute-done.3.refs_6_ = bf16[128,512]{1,0:T(8,128)(2,1)S(1)} collective-permute-done((bf16[128,512]{1,0:T(8,128)(2,1)}, bf16[128,512]{1,0:T(8,128)(2,1)S(1)}, u32[]{:S(2)}, u32[]{:S(2)}) %collective-permute-start.3) | collective-permute-done | bytes 131104 | tf_op jit(solution)/shard_map/ppermute | solution.py:571
  24.8 9.4 %collective-permute-done.17.refs_4_ = bf16[48,2048]{1,0:T(8,128)(2,1)} collective-permute-done((bf16[48,2048]{1,0:T(8,128)(2,1)}, bf16[48,2048]{1,0:T(8,128)(2,1)}, u32[]{:S(2)}, u32[]{:S(2)}) %collective-permute-start.17) | collective-permute-done | bytes 196640 | tf_op jit(solution)/shard_map/ppermute | solution.py:571
  36.0 14.1 %forward.1 = (bf16[2,1024,256]{2,1,0:T(8,128)(2,1)}, bf16[2,1024,256]{2,1,0:T(8,128)(2,1)}, bf16[2,128,1024]{2,1,0:T(8,128)(2,1)}, bf16[2,144,1024]{2,1,0:T(8,12...) custom-call(s32[1]{0:T(128)} %bitcast.refs_0_, ...), custom_call_target="tpu_custom_call" | custom-call | flops 10000000000 | bytes 20000000 | tf_op jit(solution)/shard_map/forward/pallas_call | solution.py:256
  50.2 4.7 %collective-permute-start.8 = (bf16[24,2048]{1,0:T(8,128)(2,1)}, bf16[24,2048]{1,0:T(8,128)(2,1)}, u32[]{:S(2)}, u32[]{:S(2)}) collective-permute-start(bf16[24,2048]{1,0:T(8,128)(2,1)} %get-tuple-element.43), channel_id=1, source_target_pairs={{0,2},{1,3},{2,4},{3,5},{4,6},{5,7},{6,0},{7,1},{8,10},{9,11},{10,... | collective-permute-start | bytes 294920 | tf_op jit(solution)/shard_map/ppermute | solution.py:584
  56.1 3.6 %collective-permute-done.8.refs_2_ = bf16[24,2048]{1,0:T(8,128)(2,1)} collective-permute-done((bf16[24,2048]{1,0:T(8,128)(2,1)}, bf16[24,2048]{1,0:T(8,128)(2,1)}, u32[]{:S(2)}, u32[]{:S(2)}) %collective-permute-start.8) | collective-permute-done | bytes 98336 | tf_op jit(solution)/shard_map/ppermute | solution.py:584
  64.7 6.1 %early.1 = (bf16[48,4096]{1,0:T(8,128)(2,1)}, bf16[48,4096]{1,0:T(8,128)(2,1)}, f32[96,768]{1,0:T(8,128)}) custom-call(bf16[24,2048]{1,0:T(8,128)(2,1)} %get-tuple-element.49.refs_0_, bf16[24,2048]{1,0:T(8,128)(2,1)} %collective-permute-done.14.refs_1_, bf16[48,2048]{1,0:T(8,128)(2,1)} %collective-permute-done.15.refs_2_, ...), custom_call_target="tpu_custom_call" | custom-call | flops 2000000000 | bytes 7000000 | tf_op jit(solution)/shard_map/early/pallas_call | solution.py:303
  72.7 11.7 %expert.1 = (bf16[48,4096]{1,0:T(8,128)(2,1)}, bf16[48,4096]{1,0:T(8,128)(2,1)}, bf16[24,2048]{1,0:T(8,128)(2,1)}, bf16[24,2048]{1,0:T(8,128)(2,1)}, bf16[24,204...) custom-call(bf16[24,2048]{1,0:T(8,128)(2,1)} %get-tuple-element.41.r, ...), custom_call_target="tpu_custom_call" | custom-call | flops 8000000000 | bytes 20000000 | tf_op jit(solution)/shard_map/expert/pallas_call | solution.py:368
  84.5 4.4 %collective-permute-start.22 = (bf16[24,2048]{1,0:T(8,128)(2,1)}, bf16[24,2048]{1,0:T(8,128)(2,1)}, u32[]{:S(2)}, u32[]{:S(2)}) collective-permute-start(bf16[24,2048]{1,0:T(8,128)(2,1)} %get-tuple-element.57), channel_id=1, source_target_pairs={{0,6},{1,7},{2,0},{3,1},{4,2},{5,3},{6,4},{7,5},{8,14},{9,15},{10,... | collective-permute-start | bytes 294920 | tf_op jit(solution)/shard_map/ppermute | solution.py:584
  88.9 2.4 %collective-permute-start.25 = (bf16[24,2048]{1,0:T(8,128)(2,1)}, bf16[24,2048]{1,0:T(8,128)(2,1)}, u32[]{:S(2)}, u32[]{:S(2)}) collective-permute-start(bf16[24,2048]{1,0:T(8,128)(2,1)} %get-tuple-element.60), channel_id=1, source_target_pairs={{0,5},{1,4},{2,7},{3,6},{4,1},{5,0},{6,3},{7,2},{8,13},{9,12},{10,... | collective-permute-start | bytes 294920 | tf_op jit(solution)/shard_map/ppermute | solution.py:584
  91.3 2.0 %collective-permute-start.26 = (bf16[24,2048]{1,0:T(8,128)(2,1)}, bf16[24,2048]{1,0:T(8,128)(2,1)}, u32[]{:S(2)}, u32[]{:S(2)}) collective-permute-start(bf16[24,2048]{1,0:T(8,128)(2,1)} %get-tuple-element.61), channel_id=1, source_target_pairs={{0,2},{1,3},{2,4},{3,5},{4,6},{5,7},{6,0},{7,1},{8,10},{9,11},{10,... | collective-permute-start | bytes 294920 | tf_op jit(solution)/shard_map/ppermute | solution.py:584
  94.9 10.4 %collective-permute-done.24.refs_4_ = bf16[24,2048]{1,0:T(8,128)(2,1)} collective-permute-done((bf16[24,2048]{1,0:T(8,128)(2,1)}, bf16[24,2048]{1,0:T(8,128)(2,1)}, u32[]{:S(2)}, u32[]{:S(2)}) %collective-permute-start.24) | collective-permute-done | bytes 98336 | tf_op jit(solution)/shard_map/ppermute | solution.py:584
  105.6 15.1 %backward.1 = (bf16[128,4096]{1,0:T(8,128)(2,1)}, f32[4,128,512]{2,1,0:T(8,128)}, bf16[4,128,512]{2,1,0:T(8,128)(2,1)}) custom-call(bf16[24,2048]{1,0:T(8,128)(2,1)} %get-tuple-element.55.refs_0_, bf16[24,2048]{1,0:T(8,128)(2,1)} %collective-permute-done.21.refs_1_, bf16[24,2048]{1,0:T(8,128)(2,1)} %collective-permute-done.22.refs_2_, ...), custom_call_target="tpu_custom_call" | custom-call | flops 20000000000 | bytes 20000000 | tf_op jit(solution)/shard_map/backward/pallas_call | solution.py:539
  125.5 8.1 %collective-permute-done.32.refs_2_ = bf16[48,4096]{1,0:T(8,128)(2,1)S(1)} collective-permute-done((bf16[48,4096]{1,0:T(8,128)(2,1)}, bf16[48,4096]{1,0:T(8,128)(2,1)S(1)}, u32[]{:S(2)}, u32[]{:S(2)}) %collective-permute-start.32) | collective-permute-done | bytes 393248 | tf_op jit(solution)/shard_map/ppermute | solution.py:576
  138.7 4.9 %collective-permute-done.35.refs_6_ = bf16[48,4096]{1,0:T(8,128)(2,1)S(1)} collective-permute-done((bf16[48,4096]{1,0:T(8,128)(2,1)}, bf16[48,4096]{1,0:T(8,128)(2,1)S(1)}, u32[]{:S(2)}, u32[]{:S(2)}) %collective-permute-start.35) | collective-permute-done | bytes 393248 | tf_op jit(solution)/shard_map/ppermute | solution.py:576
  143.6 1.8 collective-permute-start.31
  145.4 2.0 %collective-permute-start.30 = (bf16[128,512]{1,0:T(8,128)(2,1)S(1)}, bf16[128,512]{1,0:T(8,128)(2,1)S(1)}, u32[]{:S(2)}, u32[]{:S(2)}) collective-permute-start(bf16[128,512]{1,0:T(8,128)(2,1)S(1)} %get-tuple-element.80), channel_id=1, source_target_pairs={{0,4},{1,5},{2,6},{3,7},{4,0},{5,1},{6,2},{7,3},{8,12},{9,13},{10,... | collective-permute-start | bytes 393224 | tf_op jit(solution)/shard_map/ppermute | solution.py:571
  147.4 2.2 %collective-permute-done.38.refs_10_ = bf16[48,4096]{1,0:T(8,128)(2,1)S(1)} collective-permute-done((bf16[48,4096]{1,0:T(8,128)(2,1)}, bf16[48,4096]{1,0:T(8,128)(2,1)S(1)}, u32[]{:S(2)}, u32[]{:S(2)}) %collective-permute-start.38) | collective-permute-done | bytes 393248 | tf_op jit(solution)/shard_map/ppermute | solution.py:576
  152.5 6.8 %collective-permute-done.41.refs_14_ = bf16[48,4096]{1,0:T(8,128)(2,1)} collective-permute-done((bf16[48,4096]{1,0:T(8,128)(2,1)}, bf16[48,4096]{1,0:T(8,128)(2,1)}, u32[]{:S(2)}, u32[]{:S(2)}) %collective-permute-start.41) | collective-permute-done | bytes 393248 | tf_op jit(solution)/shard_map/ppermute | solution.py:576
  164.2 7.2 %collective-permute-done.34.refs_4_ = bf16[48,4096]{1,0:T(8,128)(2,1)S(1)} collective-permute-done((bf16[48,4096]{1,0:T(8,128)(2,1)S(1)}, bf16[48,4096]{1,0:T(8,128)(2,1)S(1)}, u32[]{:S(2)}, u32[]{:S(2)}) %collective-permute-start.34) | collective-permute-done | bytes 393248 | tf_op jit(solution)/shard_map/ppermute | solution.py:576
  172.9 4.9 %collective-permute-done.40.refs_12_ = bf16[48,4096]{1,0:T(8,128)(2,1)S(1)} collective-permute-done((bf16[48,4096]{1,0:T(8,128)(2,1)S(1)}, bf16[48,4096]{1,0:T(8,128)(2,1)S(1)}, u32[]{:S(2)}, u32[]{:S(2)}) %collective-permute-start.40) | collective-permute-done | bytes 393248 | tf_op jit(solution)/shard_map/ppermute | solution.py:576
  179.8 11.9 %grads.1 = bf16[3,192,4096]{2,1,0:T(8,128)(2,1)} custom-call(s32[1]{0:T(128)} %bitcast.19.refs_0_, bf16[48,4096]{1,0:T(8,128)(2,1)} %get-tuple-element.72.refs_1_, bf16[48,4096]{1,0:T(8,128)(2,1)} %copy-done, bf16[48,4096]{1,0:T(8,128)(2,1)} %copy-done.1, bf16[48,4096]{1,0:T(8,128)(2,1)} %copy-done.7, bf16[48,4096]{1,0:T(8,128)(2,1)} %get-tuple-element.73.refs_5_, ...), custom_call_target="tpu_custom_call" | custom-call | flops 10000000000 | bytes 15000000 | tf_op jit(solution)/shard_map/grads/pallas_call | solution.py:431
  (107 shorter events, 40.3 us)
Async XLA Ops:
  8.0 16.2 %collective-permute-start.15 = (bf16[48,2048]{1,0:T(8,128)(2,1)}, bf16[48,2048]{1,0:T(8,128)(2,1)}, u32[]{:S(2)}, u32[]{:S(2)}) collective-permute-start(bf16[48,2048]{1,0:T(8,128)(2,1)} %get-tuple-element.51), channel_id=1, source_target_pairs={{0,2},{1,3},{2,4},{3,5},{4,6},{5,7},{6,0},{7,1},{8,10},{9,11},{10,... | collective-permute-start | bytes 589832 | tf_op jit(solution)/shard_map/ppermute | solution.py:571
  9.6 14.0 %collective-permute-start.3 = (bf16[128,512]{1,0:T(8,128)(2,1)}, bf16[128,512]{1,0:T(8,128)(2,1)S(1)}, u32[]{:S(2)}, u32[]{:S(2)}) collective-permute-start(bf16[128,512]{1,0:T(8,128)(2,1)} %pad_maximum_fusion.refs_2_), channel_id=1, source_target_pairs={{0,4},{1,5},{2,6},{3,7},{4,0},{5,1},{6,2},{7,3},{8,12},{9,13},{10,... | collective-permute-start | bytes 393224 | tf_op jit(solution)/shard_map/ppermute | solution.py:571
  10.6 13.0 %collective-permute-start.5 = (bf16[128,512]{1,0:T(8,128)(2,1)}, bf16[128,512]{1,0:T(8,128)(2,1)S(1)}, u32[]{:S(2)}, u32[]{:S(2)}) collective-permute-start(bf16[128,512]{1,0:T(8,128)(2,1)} %pad_maximum_fusion.refs_2_), channel_id=1, source_target_pairs={{0,6},{1,7},{2,0},{3,1},{4,2},{5,3},{6,4},{7,5},{8,14},{9,15},{10,... | collective-permute-start | bytes 393224 | tf_op jit(solution)/shard_map/ppermute | solution.py:571
  13.5 20.7 %collective-permute-start.17 = (bf16[48,2048]{1,0:T(8,128)(2,1)}, bf16[48,2048]{1,0:T(8,128)(2,1)}, u32[]{:S(2)}, u32[]{:S(2)}) collective-permute-start(bf16[48,2048]{1,0:T(8,128)(2,1)} %get-tuple-element.52), channel_id=1, source_target_pairs={{0,4},{1,5},{2,6},{3,7},{4,0},{5,1},{6,2},{7,3},{8,12},{9,13},{10,... | collective-permute-start | bytes 589832 | tf_op jit(solution)/shard_map/ppermute | solution.py:571
  13.9 20.3 %collective-permute-start.19 = (bf16[48,2048]{1,0:T(8,128)(2,1)}, bf16[48,2048]{1,0:T(8,128)(2,1)}, u32[]{:S(2)}, u32[]{:S(2)}) collective-permute-start(bf16[48,2048]{1,0:T(8,128)(2,1)} %get-tuple-element.53), channel_id=1, source_target_pairs={{0,6},{1,7},{2,0},{3,1},{4,2},{5,3},{6,4},{7,5},{8,14},{9,15},{10,... | collective-permute-start | bytes 589832 | tf_op jit(solution)/shard_map/ppermute | solution.py:571
  34.2 16.0 %collective-permute-start.14 = (bf16[24,2048]{1,0:T(8,128)(2,1)}, bf16[24,2048]{1,0:T(8,128)(2,1)}, u32[]{:S(2)}, u32[]{:S(2)}) collective-permute-start(bf16[24,2048]{1,0:T(8,128)(2,1)} %get-tuple-element.50), channel_id=1, source_target_pairs={{0,1},{1,0},{2,3},{3,2},{4,5},{5,4},{6,7},{7,6},{8,9},{9,8},{10,11... | collective-permute-start | bytes 294920 | tf_op jit(solution)/shard_map/ppermute | solution.py:576
  34.2 25.9 %collective-permute-start.16 = (bf16[48,2048]{1,0:T(8,128)(2,1)}, bf16[48,2048]{1,0:T(8,128)(2,1)}, u32[]{:S(2)}, u32[]{:S(2)}) collective-permute-start(bf16[48,2048]{1,0:T(8,128)(2,1)} %collective-permute-done.15.refs_2_), channel_id=1, source_target_pairs={{0,1},{1,0},{2,3},{3,2},{4,5},{5,4},{6,7},{7,6},{8,9},{9,8},{10,11... | collective-permute-start | bytes 589832 | tf_op jit(solution)/shard_map/ppermute | solution.py:576
  34.7 27.1 %collective-permute-start.18 = (bf16[48,2048]{1,0:T(8,128)(2,1)}, bf16[48,2048]{1,0:T(8,128)(2,1)}, u32[]{:S(2)}, u32[]{:S(2)}) collective-permute-start(bf16[48,2048]{1,0:T(8,128)(2,1)} %collective-permute-done.17.refs_4_), channel_id=1, source_target_pairs={{0,1},{1,0},{2,3},{3,2},{4,5},{5,4},{6,7},{7,6},{8,9},{9,8},{10,11... | collective-permute-start | bytes 589832 | tf_op jit(solution)/shard_map/ppermute | solution.py:576
  34.8 28.5 %collective-permute-start.20 = (bf16[48,2048]{1,0:T(8,128)(2,1)}, bf16[48,2048]{1,0:T(8,128)(2,1)}, u32[]{:S(2)}, u32[]{:S(2)}) collective-permute-start(bf16[48,2048]{1,0:T(8,128)(2,1)} %collective-permute-done.19.refs_6_), channel_id=1, source_target_pairs={{0,1},{1,0},{2,3},{3,2},{4,5},{5,4},{6,7},{7,6},{8,9},{9,8},{10,11... | collective-permute-start | bytes 589832 | tf_op jit(solution)/shard_map/ppermute | solution.py:576
  54.9 15.9 %collective-permute-start.9 = (bf16[24,2048]{1,0:T(8,128)(2,1)}, bf16[24,2048]{1,0:T(8,128)(2,1)}, u32[]{:S(2)}, u32[]{:S(2)}) collective-permute-start(bf16[24,2048]{1,0:T(8,128)(2,1)} %get-tuple-element.44), channel_id=1, source_target_pairs={{0,3},{1,2},{2,5},{3,4},{4,7},{5,6},{6,1},{7,0},{8,11},{9,10},{10,... | collective-permute-start | bytes 294920 | tf_op jit(solution)/shard_map/ppermute | solution.py:584
  88.9 16.4 %collective-permute-start.24 = (bf16[24,2048]{1,0:T(8,128)(2,1)}, bf16[24,2048]{1,0:T(8,128)(2,1)}, u32[]{:S(2)}, u32[]{:S(2)}) collective-permute-start(bf16[24,2048]{1,0:T(8,128)(2,1)} %get-tuple-element.59), channel_id=1, source_target_pairs={{0,4},{1,5},{2,6},{3,7},{4,0},{5,1},{6,2},{7,3},{8,12},{9,13},{10,... | collective-permute-start | bytes 294920 | tf_op jit(solution)/shard_map/ppermute | solution.py:584
  88.9 16.7 %collective-permute-start.25 = (bf16[24,2048]{1,0:T(8,128)(2,1)}, bf16[24,2048]{1,0:T(8,128)(2,1)}, u32[]{:S(2)}, u32[]{:S(2)}) collective-permute-start(bf16[24,2048]{1,0:T(8,128)(2,1)} %get-tuple-element.60), channel_id=1, source_target_pairs={{0,5},{1,4},{2,7},{3,6},{4,1},{5,0},{6,3},{7,2},{8,13},{9,12},{10,... | collective-permute-start | bytes 294920 | tf_op jit(solution)/shard_map/ppermute | solution.py:584
  91.3 14.3 %collective-permute-start.26 = (bf16[24,2048]{1,0:T(8,128)(2,1)}, bf16[24,2048]{1,0:T(8,128)(2,1)}, u32[]{:S(2)}, u32[]{:S(2)}) collective-permute-start(bf16[24,2048]{1,0:T(8,128)(2,1)} %get-tuple-element.61), channel_id=1, source_target_pairs={{0,2},{1,3},{2,4},{3,5},{4,6},{5,7},{6,0},{7,1},{8,10},{9,11},{10,... | collective-permute-start | bytes 294920 | tf_op jit(solution)/shard_map/ppermute | solution.py:584
  120.7 16.0 %collective-permute-start.28 = (bf16[4,128,512]{2,1,0:T(8,128)(2,1)}, bf16[4,128,512]{2,1,0:T(8,128)(2,1)S(1)}, u32[]{:S(2)}, u32[]{:S(2)}) collective-permute-start(bf16[4,128,512]{2,1,0:T(8,128)(2,1)} %get-tuple-element.71), channel_id=1, source_target_pairs={{0,1},{1,0},{2,3},{3,2},{4,5},{5,4},{6,7},{7,6},{8,9},{9,8},{10,11... | collective-permute-start | bytes 1572872 | tf_op jit(solution)/shard_map/ppermute | solution.py:576
  124.5 19.1 %collective-permute-start.35 = (bf16[48,4096]{1,0:T(8,128)(2,1)}, bf16[48,4096]{1,0:T(8,128)(2,1)S(1)}, u32[]{:S(2)}, u32[]{:S(2)}) collective-permute-start(bf16[48,4096]{1,0:T(8,128)(2,1)} %get-tuple-element.73.refs_5_), channel_id=1, source_target_pairs={{0,16},{8,24},{16,0},{24,8},{1,17},{9,25},{17,1},{25,9},{2,18},{10... | collective-permute-start | bytes 1179656 | tf_op jit(solution)/shard_map/ppermute | solution.py:576
  125.0 20.4 %collective-permute-start.36 = (bf16[48,4096]{1,0:T(8,128)(2,1)}, bf16[48,4096]{1,0:T(8,128)(2,1)S(1)}, u32[]{:S(2)}, u32[]{:S(2)}) collective-permute-start(bf16[48,4096]{1,0:T(8,128)(2,1)} %get-tuple-element.73.refs_5_), channel_id=1, source_target_pairs={{0,8},{8,0},{16,24},{24,16},{1,9},{9,1},{17,25},{25,17},{2,10},{10... | collective-permute-start | bytes 1179656 | tf_op jit(solution)/shard_map/ppermute | solution.py:576
  133.7 16.0 %collective-permute-start.38 = (bf16[48,4096]{1,0:T(8,128)(2,1)}, bf16[48,4096]{1,0:T(8,128)(2,1)S(1)}, u32[]{:S(2)}, u32[]{:S(2)}) collective-permute-start(bf16[48,4096]{1,0:T(8,128)(2,1)} %get-tuple-element.74.refs_9_), channel_id=1, source_target_pairs={{0,8},{8,0},{16,24},{24,16},{1,9},{9,1},{17,25},{25,17},{2,10},{10... | collective-permute-start | bytes 1179656 | tf_op jit(solution)/shard_map/ppermute | solution.py:576
  135.2 16.8 %collective-permute-start.39 = (bf16[48,4096]{1,0:T(8,128)(2,1)}, bf16[48,4096]{1,0:T(8,128)(2,1)S(1)}, u32[]{:S(2)}, u32[]{:S(2)}) collective-permute-start(bf16[48,4096]{1,0:T(8,128)(2,1)} %get-tuple-element.74.refs_9_), channel_id=1, source_target_pairs={{0,16},{8,24},{16,0},{24,8},{1,17},{9,25},{17,1},{25,9},{2,18},{10... | collective-permute-start | bytes 1179656 | tf_op jit(solution)/shard_map/ppermute | solution.py:576
  136.7 22.7 %collective-permute-start.41 = (bf16[48,4096]{1,0:T(8,128)(2,1)}, bf16[48,4096]{1,0:T(8,128)(2,1)}, u32[]{:S(2)}, u32[]{:S(2)}) collective-permute-start(bf16[48,4096]{1,0:T(8,128)(2,1)} %get-tuple-element.75.refs_13_), channel_id=1, source_target_pairs={{0,16},{8,24},{16,0},{24,8},{1,17},{9,25},{17,1},{25,9},{2,18},{10... | collective-permute-start | bytes 1179656 | tf_op jit(solution)/shard_map/ppermute | solution.py:576
  143.6 17.3 %collective-permute-start.31 = (bf16[128,512]{1,0:T(8,128)(2,1)S(1)}, bf16[128,512]{1,0:T(8,128)(2,1)S(1)}, u32[]{:S(2)}, u32[]{:S(2)}) collective-permute-start(bf16[128,512]{1,0:T(8,128)(2,1)S(1)} %get-tuple-element.79), channel_id=1, source_target_pairs={{0,2},{1,3},{2,4},{3,5},{4,6},{5,7},{6,0},{7,1},{8,10},{9,11},{10,... | collective-permute-start | bytes 393224 | tf_op jit(solution)/shard_map/ppermute | solution.py:571
  145.4 16.0 %collective-permute-start.30 = (bf16[128,512]{1,0:T(8,128)(2,1)S(1)}, bf16[128,512]{1,0:T(8,128)(2,1)S(1)}, u32[]{:S(2)}, u32[]{:S(2)}) collective-permute-start(bf16[128,512]{1,0:T(8,128)(2,1)S(1)} %get-tuple-element.80), channel_id=1, source_target_pairs={{0,4},{1,5},{2,6},{3,7},{4,0},{5,1},{6,2},{7,3},{8,12},{9,13},{10,... | collective-permute-start | bytes 393224 | tf_op jit(solution)/shard_map/ppermute | solution.py:571
  149.6 12.3 %collective-permute-start.29 = (bf16[128,512]{1,0:T(8,128)(2,1)S(1)}, bf16[128,512]{1,0:T(8,128)(2,1)S(1)}, u32[]{:S(2)}, u32[]{:S(2)}) collective-permute-start(bf16[128,512]{1,0:T(8,128)(2,1)S(1)} %get-tuple-element.78), channel_id=1, source_target_pairs={{0,6},{1,7},{2,0},{3,1},{4,2},{5,3},{6,4},{7,5},{8,14},{9,15},{10,... | collective-permute-start | bytes 393224 | tf_op jit(solution)/shard_map/ppermute | solution.py:571
  161.4 16.3 %collective-permute-start.40 = (bf16[48,4096]{1,0:T(8,128)(2,1)S(1)}, bf16[48,4096]{1,0:T(8,128)(2,1)S(1)}, u32[]{:S(2)}, u32[]{:S(2)}) collective-permute-start(bf16[48,4096]{1,0:T(8,128)(2,1)S(1)} %collective-permute-done.38.refs_10_), channel_id=1, source_target_pairs={{0,16},{8,24},{16,0},{24,8},{1,17},{9,25},{17,1},{25,9},{2,18},{10... | collective-permute-start | bytes 1179656 | tf_op jit(solution)/shard_map/ppermute | solution.py:576
  161.9 17.1 %collective-permute-start.43 = (bf16[48,4096]{1,0:T(8,128)(2,1)}, bf16[48,4096]{1,0:T(8,128)(2,1)S(1)}, u32[]{:S(2)}, u32[]{:S(2)}) collective-permute-start(bf16[48,4096]{1,0:T(8,128)(2,1)} %collective-permute-done.41.refs_14_), channel_id=1, source_target_pairs={{0,8},{8,0},{16,24},{24,16},{1,9},{9,1},{17,25},{25,17},{2,10},{10... | collective-permute-start | bytes 1179656 | tf_op jit(solution)/shard_map/ppermute | solution.py:576
  (36 other events, 361.7 us)
